TPU v7x, 8 devices: a whole 2x2x1 slice. The times are simulated.
8 devices in a mesh: dp: 1 (over z), tpx: 2 (over y), tpy: 4 (over x, core).
Axes of the slice: x: 2, y: 2, z: 1, core: 2. Of those that a mesh axis runs over, the one named last changes fastest.
Arguments:
- hidden: bfloat16 [256, 4096], P('dp', ('tpx', 'tpy'))
- ln_scale: float32 [4096], P(('tpx', 'tpy'))
- w_q: bfloat16 [4096, 4096], P('tpx', 'tpy')
- w_k: bfloat16 [4096, 256], P('tpx')
- w_v: bfloat16 [4096, 256], P('tpx')
- w_gate: bfloat16 [4096, 16384], P('tpx', 'tpy')
- w_up: bfloat16 [4096, 16384], P('tpx', 'tpy')
- w_o: bfloat16 [4096, 4096], P('tpy', 'tpx')
- w_down: bfloat16 [16384, 4096], P('tpy', 'tpx')
- k_cache: bfloat16 [256, 2048, 256], P(('dp', 'tpx', 'tpy'))
- v_cache: bfloat16 [256, 2048, 256], P(('dp', 'tpx', 'tpy'))
- positions: int32 [256], P(('dp', 'tpx', 'tpy'))
Outputs:
- output 1: bfloat16 [256, 4096], P('dp', ('tpx', 'tpy'))
- output 2: bfloat16 [256, 2048, 256], P(('dp', 'tpx', 'tpy'))
- output 3: bfloat16 [256, 2048, 256], P(('dp', 'tpx', 'tpy'))
All inputs are finite; a program needn't handle non-finite values.
Results may differ from a plain program's by a relative error of at most 0.00648642.
Values are sent between devices in bfloat16 or wider.
A program may use at most 1 GiB of HBM per device.

v0:
```python
import functools

import jax
import jax.numpy as jnp
from jax import lax
from jax.experimental import pallas as pl
from jax.experimental.pallas import tpu as pltpu
from jax.sharding import PartitionSpec as P


LN_EPS = 1e-6
ROPE_BASE = 10000.0
MESH = pl.DeviceIdType.MESH
F32 = jnp.float32
BF16 = jnp.bfloat16


def rope_tables(positions, head_dim):
    half_dim = head_dim // 2
    inv_freq = ROPE_BASE ** (-(jnp.arange(half_dim, dtype=F32) * 2.0 / head_dim))
    angles = positions.astype(F32)[:, None] * inv_freq[None, :]
    return jnp.cos(angles), jnp.sin(angles)


def rope(x, cos, sin):
    half = x.shape[-1] // 2
    lead, tail = x[:, :half], x[:, half:]
    return jnp.concatenate([lead * cos - tail * sin, lead * sin + tail * cos], axis=-1)


def front_kernel(nx, ny, h_ref, sc_ref, u_ref, hbuf, scbuf, stat, hs, hr, ss, sr, ts, tr):
    ix, iy = lax.axis_index("tpx"), lax.axis_index("tpy")
    rows, width = h_ref.shape
    partner = iy + 1 - 2 * lax.rem(iy, 2)
    cross = lax.rem(iy + 2, ny)
    diag = lax.rem(partner + 2, ny)
    me = ix * ny + iy

    barrier = pltpu.get_barrier_semaphore()
    for dx in range(nx):
        for dy in range(ny):
            if dx or dy:
                pl.semaphore_signal(
                    barrier,
                    inc=1,
                    device_id={"tpx": lax.rem(ix + dx, nx), "tpy": lax.rem(iy + dy, ny)},
                    device_id_type=MESH,
                )
    pl.semaphore_wait(barrier, nx * ny - 1)

    half = rows // 2

    def block_copy(src, owner, part, dst_y, k):
        sl = pl.ds(part * half, half)
        return pltpu.make_async_remote_copy(
            src_ref=src.at[sl],
            dst_ref=hbuf.at[owner, sl],
            send_sem=hs.at[k, part],
            recv_sem=hr.at[k, part],
            device_id={"tpx": ix, "tpy": dst_y},
            device_id_type=MESH,
        )

    to_cross = [block_copy(h_ref, iy, p, cross, 0) for p in range(2)]
    to_partner = [block_copy(h_ref, iy, p, partner, 1) for p in range(2)]
    for c in to_cross + to_partner:
        c.start()
    sc_copies = []
    for k, dst in enumerate((cross, partner, diag)):
        c = pltpu.make_async_remote_copy(
            src_ref=sc_ref,
            dst_ref=scbuf.at[iy],
            send_sem=ss.at[k],
            recv_sem=sr.at[k],
            device_id={"tpx": ix, "tpy": dst},
            device_id_type=MESH,
        )
        c.start()
        sc_copies.append(c)

    hf = h_ref[...].astype(F32)
    total = jnp.sum(hf, axis=1, keepdims=True)
    dev = hf - total / width
    spread = jnp.sum(dev * dev, axis=1, keepdims=True)
    lane = lax.broadcasted_iota(jnp.int32, (rows, 128), 1)
    packed = jnp.where(lane == 0, total, jnp.where(lane == 1, spread, 0.0))
    stat[me] = jnp.transpose(packed)[:8]

    stat_copies = []
    k = 0
    for dx in range(nx):
        for dy in range(ny):
            if dx or dy:
                c = pltpu.make_async_remote_copy(
                    src_ref=stat.at[me],
                    dst_ref=stat.at[me],
                    send_sem=ts.at[k],
                    recv_sem=tr.at[k],
                    device_id={"tpx": lax.rem(ix + dx, nx), "tpy": lax.rem(iy + dy, ny)},
                    device_id_type=MESH,
                )
                c.start()
                stat_copies.append(c)
                k += 1

    forward = []
    for p in range(2):
        to_cross[p].wait_recv()
        c = pltpu.make_async_remote_copy(
            src_ref=hbuf.at[cross, pl.ds(p * half, half)],
            dst_ref=hbuf.at[cross, pl.ds(p * half, half)],
            send_sem=hs.at[2, p],
            recv_sem=hr.at[2, p],
            device_id={"tpx": ix, "tpy": partner},
            device_id_type=MESH,
        )
        c.start()
        forward.append(c)

    for c in stat_copies:
        c.wait_recv()
    n_dev = nx * ny
    sums = [stat[d, 0:1, :] for d in range(n_dev)]
    sprd = [stat[d, 1:2, :] for d in range(n_dev)]
    mean = functools.reduce(jnp.add, sums) / (width * n_dev)
    m2 = functools.reduce(jnp.add, sprd)
    for d in range(n_dev):
        gap = sums[d] / width - mean
        m2 = m2 + width * gap * gap
    var = m2 / (width * n_dev)
    rs = lax.rsqrt(var + LN_EPS)
    sub = lax.broadcasted_iota(jnp.int32, (128, rows), 0)
    cols = jnp.transpose(jnp.where(sub == 0, mean, jnp.where(sub == 1, rs, 0.0)))
    mean_c, rs_c = cols[:, 0:1], cols[:, 1:2]

    def emit(block, scale, owner):
        u = ((block.astype(F32) - mean_c) * rs_c * scale).astype(BF16)
        col = pl.ds(pl.multiple_of(owner * width, width), width)
        for hf_i in range(2):
            pos = lax.rem(hf_i + ix + 1, 2)
            u_ref[pl.ds(pl.multiple_of(pos * half, half), half), col] = u[hf_i * half : (hf_i + 1) * half]

    emit(h_ref[...], sc_ref[...], iy)
    for c in sc_copies:
        c.wait_recv()
    for c in to_partner:
        c.wait_recv()
    emit(hbuf[partner], scbuf[partner], partner)
    emit(hbuf[cross], scbuf[cross], cross)
    for c in forward:
        c.wait_recv()
    emit(hbuf[diag], scbuf[diag], diag)
    for c in to_cross + to_partner + forward + sc_copies + stat_copies:
        c.wait_send()


def front(nx, ny, hidden, ln_scale):
    rows, width = hidden.shape
    n_dev = nx * ny
    return pl.pallas_call(
        functools.partial(front_kernel, nx, ny),
        out_shape=jax.ShapeDtypeStruct((rows, width * ny), BF16),
        in_specs=[pl.BlockSpec(memory_space=pltpu.VMEM)] * 2,
        out_specs=pl.BlockSpec(memory_space=pltpu.VMEM),
        scratch_shapes=[
            pltpu.VMEM((ny, rows, width), BF16),
            pltpu.VMEM((ny, 1, width), F32),
            pltpu.VMEM((n_dev, 8, rows), F32),
            pltpu.SemaphoreType.DMA((3, 2)),
            pltpu.SemaphoreType.DMA((3, 2)),
            pltpu.SemaphoreType.DMA((3,)),
            pltpu.SemaphoreType.DMA((3,)),
            pltpu.SemaphoreType.DMA((n_dev - 1,)),
            pltpu.SemaphoreType.DMA((n_dev - 1,)),
        ],
        compiler_params=pltpu.CompilerParams(collective_id=0, has_side_effects=True),
        cost_estimate=pl.CostEstimate(flops=10**9, bytes_accessed=2 * 10**6, transcendentals=0),
        name="front",
    )(hidden, ln_scale.reshape(1, width))


def gu_kernel(u_ref, wg_ref, wu_ref, send, keep):
    half = u_ref.shape[0] // 2
    for k, w_ref in enumerate((wg_ref, wu_ref)):
        y = jnp.dot(u_ref[...], w_ref[...], preferred_element_type=F32)
        send[k] = y[:half]
        keep[k] = y[half:]


def gate_up(u, w_gate, w_up, start, cols, blk):
    rows, kdim = u.shape
    half = rows // 2
    first = start // blk
    shape = jax.ShapeDtypeStruct((2, half, cols), F32)
    wspec = pl.BlockSpec((kdim, blk), lambda i: (0, i + first))
    ospec = pl.BlockSpec((2, half, blk), lambda i: (0, 0, i))
    return pl.pallas_call(
        gu_kernel,
        grid=(cols // blk,),
        out_shape=[shape, shape],
        in_specs=[pl.BlockSpec((rows, kdim), lambda i: (0, 0)), wspec, wspec],
        out_specs=[ospec, ospec],
        compiler_params=pltpu.CompilerParams(vmem_limit_bytes=56 * 2**20),
        cost_estimate=pl.CostEstimate(
            flops=4 * rows * kdim * cols, bytes_accessed=4 * kdim * cols, transcendentals=0
        ),
        name="gate_up",
    )(u, w_gate, w_up)


def attn_kernel(nb, ahead, pos_ref, q_ref, kn_ref, vn_ref, cos_ref, sin_ref, kc_ref, vc_ref,
                o_ref, ko_ref, vo_ref, kbuf, vbuf, krow, vrow, ki, vi, ks, vs):
    n_seq, n_head, dim = q_ref.shape
    length = kbuf.shape[1]

    def fetch(b, slot):
        pltpu.make_async_copy(kc_ref.at[b], kbuf.at[slot], ki.at[slot]).start()
        pltpu.make_async_copy(vc_ref.at[b], vbuf.at[slot], vi.at[slot]).start()

    def wait_out(b, slot):
        pltpu.make_async_copy(kbuf.at[slot], ko_ref.at[b], ks.at[slot]).wait()
        pltpu.make_async_copy(vbuf.at[slot], vo_ref.at[b], vs.at[slot]).wait()

    for b in range(ahead):
        fetch(b, b)
    krow[...] = rope(kn_ref[...].astype(F32), cos_ref[...], sin_ref[...]).astype(BF16).astype(F32)
    vrow[...] = vn_ref[...].astype(F32)

    def patch(buf, slot, row, p):
        base = pl.multiple_of((p // 16) * 16, 16)
        old = buf[slot, pl.ds(base, 16), :].astype(F32)
        hit = lax.broadcasted_iota(jnp.int32, old.shape, 0) == p - base
        buf[slot, pl.ds(base, 16), :] = jnp.where(hit, row, old).astype(BF16)

    @pl.loop(0, n_seq // 2)
    def _(i):
        work = []
        for j in range(2):
            b = 2 * i + j
            slot = lax.rem(b, nb)
            nxt = b + ahead
            nslot = lax.rem(nxt, nb)

            @pl.when(jnp.logical_and(nxt < n_seq, nxt >= nb))
            def _():
                wait_out(nxt - nb, nslot)

            @pl.when(nxt < n_seq)
            def _():
                fetch(nxt, nslot)

            work.append((b, slot))
        for b, slot in work:
            p = pos_ref[b]
            pltpu.make_async_copy(kc_ref.at[b], kbuf.at[slot], ki.at[slot]).wait()
            patch(kbuf, slot, krow[pl.ds(b, 1), :], p)
            pltpu.make_async_copy(vc_ref.at[b], vbuf.at[slot], vi.at[slot]).wait()
            patch(vbuf, slot, vrow[pl.ds(b, 1), :], p)
        for b, slot in work:
            p = pos_ref[b]
            q = rope(q_ref[b].astype(F32), cos_ref[pl.ds(b, 1), :], sin_ref[pl.ds(b, 1), :]).astype(BF16)
            s = lax.dot_general(q, kbuf[slot], (((1,), (1,)), ((), ())), preferred_element_type=F32)
            s = s * (dim ** -0.5)
            ok = lax.broadcasted_iota(jnp.int32, (n_head, length), 1) <= p
            s = jnp.where(ok, s, -jnp.inf)
            e = jnp.exp(s - jnp.max(s, axis=1, keepdims=True))
            prob = (e / jnp.sum(e, axis=1, keepdims=True)).astype(BF16)
            o = jnp.dot(prob, vbuf[slot], preferred_element_type=F32)
            o_ref[b] = o.astype(BF16)
        for b, slot in work:
            pltpu.make_async_copy(kbuf.at[slot], ko_ref.at[b], ks.at[slot]).start()
            pltpu.make_async_copy(vbuf.at[slot], vo_ref.at[b], vs.at[slot]).start()

    for b in range(n_seq - nb, n_seq):
        wait_out(b, b % nb)


def attention(q, k_new, v_new, cos, sin, k_cache, v_cache, positions, nb=8, ahead=4):
    n_seq, length, dim = k_cache.shape
    n_head = q.shape[1]
    vm = pl.BlockSpec(memory_space=pltpu.VMEM)
    hbm = pl.BlockSpec(memory_space=pltpu.HBM)
    return pl.pallas_call(
        functools.partial(attn_kernel, nb, ahead),
        out_shape=[
            jax.ShapeDtypeStruct(q.shape, BF16),
            jax.ShapeDtypeStruct(k_cache.shape, BF16),
            jax.ShapeDtypeStruct(v_cache.shape, BF16),
        ],
        in_specs=[pl.BlockSpec(memory_space=pltpu.SMEM), vm, vm, vm, vm, vm, hbm, hbm],
        out_specs=[vm, hbm, hbm],
        scratch_shapes=[
            pltpu.VMEM((nb, length, dim), BF16),
            pltpu.VMEM((nb, length, dim), BF16),
            pltpu.VMEM((n_seq, dim), F32),
            pltpu.VMEM((n_seq, dim), F32),
            pltpu.SemaphoreType.DMA((nb,)),
            pltpu.SemaphoreType.DMA((nb,)),
            pltpu.SemaphoreType.DMA((nb,)),
            pltpu.SemaphoreType.DMA((nb,)),
        ],
        compiler_params=pltpu.CompilerParams(vmem_limit_bytes=56 * 2**20),
        cost_estimate=pl.CostEstimate(
            flops=4 * 10**10, bytes_accessed=8 * n_seq * length * dim, transcendentals=n_seq * n_head * length
        ),
        name="attention",
    )(positions, q, k_new, v_new, cos, sin, k_cache, v_cache)


def tail_kernel(n_gu, cuts, n_w, *refs):
    keeps, recvs = refs[:n_gu], refs[n_gu : 2 * n_gu]
    (o_ref, h_ref, wd_hbm, wo_hbm, out_ref, wd, kbuf, rbuf, aown, aoth, give, hold, got1, pass_, got2,
     wsem, ksem, rsem, as_, ar, s1, r1, s2, r2) = refs[2 * n_gu :]
    ix, iy = lax.axis_index("tpx"), lax.axis_index("tpy")
    half = aown.shape[0]
    gcols = kbuf.shape[3]
    width = h_ref.shape[1]
    kact, ko = wd_hbm.shape[0], wo_hbm.shape[0]
    partner = iy + 1 - 2 * lax.rem(iy, 2)
    cross = lax.rem(iy + 2, 4)
    core, chip = lax.rem(iy, 2), iy // 2
    peer_x = {"tpx": 1 - ix, "tpy": iy}
    peer_core = {"tpx": ix, "tpy": partner}
    peer_chip = {"tpx": ix, "tpy": cross}

    gu_loads = []
    for r, (r0, rn) in enumerate(cuts):
        group = []
        rows = pl.ds(r0, rn)
        for g in range(n_gu):
            group.append(pltpu.make_async_copy(keeps[g].at[:, rows], kbuf.at[g, :, rows], ksem.at[r, g]))
            group.append(pltpu.make_async_copy(recvs[g].at[:, rows], rbuf.at[g, :, rows], rsem.at[r, g]))
        for c in group:
            c.start()
        gu_loads.append(group)
    step = kact // n_w
    w_loads = []
    for j in range(n_w + 1):
        if j < n_w:
            src, dst = wd_hbm.at[pl.ds(j * step, step)], wd.at[pl.ds(j * step, step)]
        else:
            src, dst = wo_hbm, wd.at[pl.ds(kact, ko)]
        c = pltpu.make_async_copy(src, dst, wsem.at[j])
        c.start()
        w_loads.append(c)

    barrier = pltpu.get_barrier_semaphore()
    for d in (peer_x, peer_core, peer_chip):
        pl.semaphore_signal(barrier, inc=1, device_id=d, device_id_type=MESH)
    pl.semaphore_wait(barrier, 3)

    sends = []
    for r, (r0, rn) in enumerate(cuts):
        rows = pl.ds(r0, rn)
        for c in gu_loads[r]:
            c.wait()
        for g in range(n_gu):
            gate = (kbuf[g, 0, rows, :] + rbuf[g, 0, rows, :]).astype(BF16).astype(F32)
            up = (kbuf[g, 1, rows, :] + rbuf[g, 1, rows, :]).astype(BF16).astype(F32)
            aown[rows, g * gcols : (g + 1) * gcols] = (jax.nn.silu(gate) * up).astype(BF16)
        aown[rows, kact:] = o_ref[rows, :]
        c = pltpu.make_async_remote_copy(
            src_ref=aown.at[rows],
            dst_ref=aoth.at[rows],
            send_sem=as_.at[r],
            recv_sem=ar.at[r],
            device_id=peer_x,
            device_id_type=MESH,
        )
        c.start()
        sends.append(c)
    for c in w_loads:
        c.wait()

    blocks = [(half, half)] + [(r0, rn) for r0, rn in cuts]

    def product(lhs, x, c):
        col = pl.ds(pl.multiple_of((x * 2 + c) * width, width), width)
        return jnp.dot(lhs, wd[:, col], preferred_element_type=F32)

    stage1, stage2 = [], []

    def run_block(k):
        r0, rn = blocks[k]
        rows = pl.ds(r0, rn)
        if k == 0:
            lhs = aown[...]
        else:
            sends[k - 1].wait_recv()
            lhs = aoth[rows, :]
        for x in range(2):
            give[x, rows, :] = product(lhs, x, 1 - core)
        c = pltpu.make_async_remote_copy(
            src_ref=give.at[:, rows],
            dst_ref=got1.at[:, rows],
            send_sem=s1.at[k],
            recv_sem=r1.at[k],
            device_id=peer_core,
            device_id_type=MESH,
        )
        c.start()
        stage1.append(c)
        hold[0, rows, :] = product(lhs, 1 - chip, core)
        hold[1, rows, :] = product(lhs, chip, core)

    def reduce_block(k):
        r0, rn = blocks[k]
        rows = pl.ds(r0, rn)
        stage1[k].wait_recv()
        pass_[rows, :] = hold[0, rows, :] + got1[1 - chip, rows, :]
        c = pltpu.make_async_remote_copy(
            src_ref=pass_.at[rows],
            dst_ref=got2.at[rows],
            send_sem=s2.at[k],
            recv_sem=r2.at[k],
            device_id=peer_chip,
            device_id_type=MESH,
        )
        c.start()
        stage2.append(c)

    def finish_block(k):
        r0, rn = blocks[k]
        rows = pl.ds(r0, rn)
        stage2[k].wait_recv()
        total = hold[1, rows, :] + got1[chip, rows, :] + got2[rows, :]
        base = ix * half if k == 0 else (1 - ix) * half + r0
        nat = pl.ds(pl.multiple_of(base, 32), rn)
        out_ref[nat, :] = (h_ref[nat, :].astype(F32) + total).astype(BF16)

    n_blk = len(blocks)
    for k in range(n_blk):
        run_block(k)
        if k:
            reduce_block(k - 1)
    reduce_block(n_blk - 1)
    for k in range(n_blk):
        finish_block(k)
    for c in sends + stage1 + stage2:
        c.wait_send()


def tail(keeps, recvs, o_own, hidden, w_down, w_o):
    rows, width = hidden.shape
    n_gu = len(keeps)
    _, half, gcols = keeps[0].shape
    n = w_down.shape[1]
    kdim = w_down.shape[0] + w_o.shape[0]
    cuts = [(0, 64), (64, 32), (96, 32)]
    n_w, n_cut, n_blk = 8, len(cuts), len(cuts) + 1
    vm = pl.BlockSpec(memory_space=pltpu.VMEM)
    anywhere = pl.BlockSpec(memory_space=pl.ANY)
    dma = pltpu.SemaphoreType.DMA
    return pl.pallas_call(
        functools.partial(tail_kernel, n_gu, cuts, n_w),
        out_shape=jax.ShapeDtypeStruct((rows, width), BF16),
        in_specs=[anywhere] * (2 * n_gu) + [vm, vm] + [pl.BlockSpec(memory_space=pltpu.HBM)] * 2,
        out_specs=vm,
        scratch_shapes=[
            pltpu.VMEM((kdim, n), BF16),
            pltpu.VMEM((n_gu, 2, half, gcols), F32),
            pltpu.VMEM((n_gu, 2, half, gcols), F32),
            pltpu.VMEM((half, kdim), BF16),
            pltpu.VMEM((half, kdim), BF16),
            pltpu.VMEM((2, rows, width), F32),
            pltpu.VMEM((2, rows, width), F32),
            pltpu.VMEM((2, rows, width), F32),
            pltpu.VMEM((rows, width), F32),
            pltpu.VMEM((rows, width), F32),
            dma((n_w + 1,)),
            dma((n_cut, n_gu)),
            dma((n_cut, n_gu)),
            dma((n_cut,)),
            dma((n_cut,)),
            dma((n_blk,)),
            dma((n_blk,)),
            dma((n_blk,)),
            dma((n_blk,)),
        ],
        compiler_params=pltpu.CompilerParams(collective_id=1, has_side_effects=True, vmem_limit_bytes=56 * 2**20),
        cost_estimate=pl.CostEstimate(flops=2 * rows * kdim * n, bytes_accessed=2 * kdim * n, transcendentals=0),
        name="tail",
    )(*keeps, *recvs, o_own, hidden, w_down, w_o)


def solution(mesh):
    x_size = mesh.shape["tpx"]
    y_size = mesh.shape["tpy"]
    hidden_spec = P("dp", ("tpx", "tpy"))
    cache_spec = P(("dp", "tpx", "tpy"), None, None)
    in_specs = (hidden_spec, P(("tpx", "tpy")), P("tpx", "tpy"), P("tpx", None), P("tpx", None), P("tpx", "tpy"), P("tpx", "tpy"), P("tpy", "tpx"), P("tpy", "tpx"), cache_spec, cache_spec, P(("dp", "tpx", "tpy")))
    out_specs = (hidden_spec, cache_spec, cache_spec)
    swap_x = [(0, 1), (1, 0)]
    n_chunk = 4

    def device_step(hidden, ln_scale, w_q, w_k, w_v, w_gate, w_up, w_o, w_down, k_cache, v_cache, positions):
        iy = lax.axis_index("tpy")
        rows, _ = hidden.shape
        half = rows // 2
        n_seq = positions.shape[0]
        dim = k_cache.shape[2]
        cols = w_gate.shape[1]

        def dot(a, b):
            return jnp.dot(a, b, preferred_element_type=F32)

        u = front(x_size, y_size, hidden, ln_scale)
        u_oth, u_own = u[:half], u[half:]
        q_send = dot(u_oth, w_q)
        kv_rows_oth = lax.dynamic_slice_in_dim(u_oth, iy * n_seq, n_seq, axis=0)
        kv_rows_own = lax.dynamic_slice_in_dim(u_own, iy * n_seq, n_seq, axis=0)
        kv_send = jnp.concatenate([dot(kv_rows_oth, w_k), dot(kv_rows_oth, w_v)], axis=1)
        q_recv = lax.ppermute(q_send, "tpx", swap_x)
        kv_recv = lax.ppermute(kv_send, "tpx", swap_x)

        per = cols // n_chunk
        keep, recv = [], []
        for c in range(n_chunk):
            s, k = gate_up(u, w_gate, w_up, c * per, per, 512)
            keep.append(k)
            recv.append(lax.ppermute(s, "tpx", swap_x))

        q_own = dot(u_own, w_q)
        kv_own = jnp.concatenate([dot(kv_rows_own, w_k), dot(kv_rows_own, w_v)], axis=1)
        q_heads = (q_own + q_recv).astype(BF16).reshape(half, -1, dim)
        kv_new = (kv_own + kv_recv).astype(BF16)
        q_seq = lax.all_to_all(q_heads, "tpy", 0, 1, tiled=True)
        cos_tab, sin_tab = rope_tables(positions, dim)
        attn_seq, k_all, v_all = attention(q_seq, kv_new[:, :dim], kv_new[:, dim:], cos_tab, sin_tab, k_cache, v_cache, positions)

        attn_heads = lax.all_to_all(attn_seq, "tpy", 1, 0, tiled=True)
        o_own = attn_heads.reshape(half, -1)
        hidden_out = tail(keep, recv, o_own, hidden, w_down, w_o)
        return hidden_out, k_all, v_all

    return jax.shard_map(device_step, mesh=mesh, in_specs=in_specs, out_specs=out_specs, check_vma=False)
```

profile of v0, /device:TPU:0, one launch (start us, length us, event | category | flops | bytes accessed | tf_op | source)
XLA Modules:
  0.0 170.6 jit_solution(5104980436224745046)
XLA Ops:
  0.6 0.0 copy-start
  0.6 15.1 %front.1.u_ref = bf16[256,2048]{1,0:T(8,128)(2,1)} custom-call(bf16[256,512]{1,0:T(8,128)(2,1)} %refs_9_.1, f32[1,512]{1,0:T(1,128)} %bitcast.19), custom_call_target="tpu_custom_call" | custom-call | flops 1000000000 | bytes 2000000 | tf_op jit(solution)/shard_map/front/pallas_call | solution.py:160
  15.8 0.0 copy-start.2
  15.8 0.0 copy-start.5
  15.8 4.0 %fusion.14 = f32[128,1024]{1,0:T(8,128)} fusion(bf16[2048,1024]{1,0:T(8,128)(2,1)} %param.14, bf16[256,2048]{1,0:T(8,128)(2,1)} %front.1.u_ref), kind=kOutput, calls=%fused_computation.20 | convolution fusion | flops 536870912 | bytes 5242880 | tf_op jit(solution)/shard_map/dot_general | solution.py:505
  19.8 1.4 collective-permute-start.4
  21.2 0.0 copy-done.2
  21.2 0.1 fusion.17
  21.3 0.0 copy-done
  21.3 0.3 fusion.3
  21.6 0.0 copy-done.5
  21.6 0.3 fusion.1
  21.9 0.7 collective-permute-start.5
  22.5 6.1 %gate_up.7 = (f32[2,128,1024]{2,1,0:T(8,128)}, f32[2,128,1024]{2,1,0:T(8,128)}) custom-call(bf16[256,2048]{1,0:T(8,128)(2,1)} %front.1.u_ref, bf16[2048,4096]{1,0:T(8,128)(2,1)} %wg_ref.7, bf16[2048,4096]{1,0:T(8,128)(2,1)} %wu_ref.7), custom_call_target="tpu_custom_call" | custom-call | flops 2147483648 | bytes 8388608 | tf_op jit(solution)/shard_map/gate_up/pallas_call | solution.py:197
  28.6 1.4 collective-permute-start.3
  30.0 6.1 %gate_up.6 = (f32[2,128,1024]{2,1,0:T(8,128)}, f32[2,128,1024]{2,1,0:T(8,128)}) custom-call(bf16[256,2048]{1,0:T(8,128)(2,1)} %front.1.u_ref, bf16[2048,4096]{1,0:T(8,128)(2,1)} %wg_ref.7, bf16[2048,4096]{1,0:T(8,128)(2,1)} %wu_ref.7), custom_call_target="tpu_custom_call" | custom-call | flops 2147483648 | bytes 8388608 | tf_op jit(solution)/shard_map/gate_up/pallas_call | solution.py:197
  36.1 0.6 collective-permute-start.2
  36.7 6.6 %gate_up.4 = (f32[2,128,1024]{2,1,0:T(8,128)}, f32[2,128,1024]{2,1,0:T(8,128)}) custom-call(bf16[256,2048]{1,0:T(8,128)(2,1)} %front.1.u_ref, bf16[2048,4096]{1,0:T(8,128)(2,1)} %wg_ref.7, bf16[2048,4096]{1,0:T(8,128)(2,1)} %wu_ref.7), custom_call_target="tpu_custom_call" | custom-call | flops 2147483648 | bytes 8388608 | tf_op jit(solution)/shard_map/gate_up/pallas_call | solution.py:197
  43.3 1.4 collective-permute-start
  44.8 0.3 fusion.7
  45.0 0.3 fusion.5
  45.3 0.0 copy-done.7
  45.4 0.7 multiply_sine_fusion
  46.1 6.2 %gate_up.5 = (f32[2,128,1024]{2,1,0:T(8,128)}, f32[2,128,1024]{2,1,0:T(8,128)}) custom-call(bf16[256,2048]{1,0:T(8,128)(2,1)} %front.1.u_ref, bf16[2048,4096]{1,0:T(8,128)(2,1)} %wg_ref.7, bf16[2048,4096]{1,0:T(8,128)(2,1)} %wu_ref.7), custom_call_target="tpu_custom_call" | custom-call | flops 2147483648 | bytes 8388608 | tf_op jit(solution)/shard_map/gate_up/pallas_call | solution.py:197
  52.3 0.0 collective-permute-done.5
  52.3 0.6 collective-permute-start.1
  53.0 0.0 collective-permute-done.4
  53.0 0.0 copy-done.3
  53.0 0.0 copy-done.4
  53.0 1.8 %fusion = bf16[128,1024]{1,0:T(8,128)(2,1)S(1)} fusion(f32[128,1024]{1,0:T(8,128)} %collective-permute-done.4, bf16[2048,1024]{1,0:T(8,128)(2,1)S(1)} %copy-done.4, bf16[256,2048]{1,0:T(8,128)(2,1)S(1)} %copy-done.3), kind=kOutput, calls=%fused_computation.1 | convolution fusion | flops 537133056 | bytes 5505024 | tf_op jit(solution)/shard_map/dot_general | solution.py:505
  54.8 0.9 reshape.24
  55.6 3.4 %all-to-all-start = ((bf16[128,4,256]{2,1,0:T(4,128)(2,1)}), bf16[128,4,256]{2,1,0:T(4,128)(2,1)S(1)}, u32[]{:S(2)}, u32[]{:S(2)}) async-start(bf16[128,4,256]{2,1,0:T(4,128)(2,1)} %reshape.24), calls=%async_computation | async-start | bytes 524288 | tf_op jit(solution)/shard_map/all_to_all | solution.py:527
  59.1 0.6 fusion.18
  59.7 5.4 %all-to-all-done = bf16[128,4,256]{2,1,0:T(4,128)(2,1)S(1)} async-done(((bf16[128,4,256]{2,1,0:T(4,128)(2,1)}), bf16[128,4,256]{2,1,0:T(4,128)(2,1)S(1)}, u32[]{:S(2)}, u32[]{:S(2)}) %all-to-all-start) | async-done | bytes 262176 | tf_op jit(solution)/shard_map/all_to_all | solution.py:527
  65.1 0.2 copy.20
  65.3 0.8 all_to_all.27.q_ref
  66.0 45.4 %attention.1 = (bf16[32,16,256]{2,1,0:T(8,128)(2,1)}, bf16[32,2048,256]{2,1,0:T(8,128)(2,1)}, bf16[32,2048,256]{2,1,0:T(8,128)(2,1)}) custom-call(s32[32]{0:T(128)} %pos_ref.1, bf16[32,16,256]{2,1,0:T(8,128)(2,1)} %all_to_all.27.q_ref, bf16[32,256]{1,0:T(8,128)(2,1)} %get-tuple-element.28.kn_ref, bf16[32,256]{1,0:T(8,128)(2,1)} %get-tuple-element.27.vn_ref, ...), custom_call_target="tpu_custom_call" | custom-call | flops 40000000000 | bytes 134217728 | tf_op jit(solution)/shard_map/attention/pallas_call | solution.py:283
  111.4 1.0 copy.21
  112.4 8.4 %all_to_all.33 = bf16[32,16,256]{2,0,1:T(8,128)(2,1)S(1)} all-to-all(bf16[32,16,256]{2,0,1:T(8,128)(2,1)S(1)} %copy.21), channel_id=1, replica_groups=mesh['dp'=1,'tpx'=2,'tpy'=4] {'tpy'}, dimensions={1} | all-to-all | bytes 524288 | tf_op jit(solution)/shard_map/all_to_all | solution.py:531
  120.8 0.2 copy.22
  121.0 0.7 copy.23
  121.8 0.0 collective-permute-done.3.refs_7_
  121.8 0.0 collective-permute-done.2.refs_6_
  121.8 0.0 collective-permute-done.refs_4_
  121.8 3.8 %collective-permute-done.1.refs_5_ = f32[2,128,1024]{2,1,0:T(8,128)S(1)} collective-permute-done((f32[2,128,1024]{2,1,0:T(8,128)}, f32[2,128,1024]{2,1,0:T(8,128)S(1)}, u32[]{:S(2)}, u32[]{:S(2)}) %collective-permute-start.1) | collective-permute-done | bytes 1048608 | tf_op jit(solution)/shard_map/ppermute | solution.py:521
  125.6 1.1 copy-done.6
  126.6 42.3 %tail.1 = bf16[256,512]{1,0:T(8,128)(2,1)} custom-call(f32[2,128,1024]{2,1,0:T(8,128)} %get-tuple-element.14.refs_0_, f32[2,128,1024]{2,1,0:T(8,128)} %get-tuple-element.15.refs_1_, f32[2,128,1024]{2,1,0:T(8,128)} %get-tuple-element.16.refs_2_, f32[2,128,1024]{2,1,0:T(8,128)} %get-tuple-element.17.refs_3_, f32[2,128,1024]{2,1,0:T(8,128)} %collective-permute-done.refs_4_, ...), custom_call_target="tpu_custom_call" | custom-call | flops 5368709120 | bytes 20971520 | tf_op jit(solution)/shard_map/tail/pallas_call | solution.py:454
  168.9 1.7 copy.25
  (11 shorter events, 0.1 us)
Async XLA Ops:
  0.6 20.6 %copy-start = (bf16[2048,256]{1,0:T(8,128)(2,1)S(1)}, bf16[2048,256]{1,0:T(8,128)(2,1)}, u32[]{:S(2)}) copy-start(bf16[2048,256]{1,0:T(8,128)(2,1)} %param.15) | copy-start | bytes 3145732
  15.8 5.4 %copy-start.2 = (bf16[256,2048]{1,0:T(8,128)(2,1)S(1)}, bf16[256,2048]{1,0:T(8,128)(2,1)}, u32[]{:S(2)}) copy-start(bf16[256,2048]{1,0:T(8,128)(2,1)} %front.1.u_ref) | copy-start | bytes 3145732
  15.8 5.8 %copy-start.5 = (bf16[2048,256]{1,0:T(8,128)(2,1)S(1)}, bf16[2048,256]{1,0:T(8,128)(2,1)}, u32[]{:S(2)}) copy-start(bf16[2048,256]{1,0:T(8,128)(2,1)} %param.16) | copy-start | bytes 3145732
  19.8 33.2 %collective-permute-start.4 = (f32[128,1024]{1,0:T(8,128)}, f32[128,1024]{1,0:T(8,128)}, u32[]{:S(2)}, u32[]{:S(2)}) collective-permute-start(f32[128,1024]{1,0:T(8,128)} %fusion.14), channel_id=1, source_target_pairs={{0,4},{4,0},{1,5},{5,1},{2,6},{6,2},{3,7},{7,3}} | collective-permute-start | bytes 1572872 | tf_op jit(solution)/shard_map/ppermute | solution.py:513
  21.9 30.4 %collective-permute-start.5 = (f32[32,512]{1,0:T(8,128)S(1)}, f32[32,512]{1,0:T(8,128)S(1)}, u32[]{:S(2)}, u32[]{:S(2)}) collective-permute-start(f32[32,512]{1,0:T(8,128)S(1)} %pad_maximum_fusion), channel_id=1, source_target_pairs={{0,4},{4,0},{1,5},{5,1},{2,6},{6,2},{3,7},{7,3}} | collective-permute-start | bytes 196616 | tf_op jit(solution)/shard_map/ppermute | solution.py:514
  28.6 93.2 %collective-permute-start.3 = (f32[2,128,1024]{2,1,0:T(8,128)}, f32[2,128,1024]{2,1,0:T(8,128)}, u32[]{:S(2)}, u32[]{:S(2)}) collective-permute-start(f32[2,128,1024]{2,1,0:T(8,128)} %get-tuple-element.21), channel_id=1, source_target_pairs={{0,4},{4,0},{1,5},{5,1},{2,6},{6,2},{3,7},{7,3}} | collective-permute-start | bytes 3145736 | tf_op jit(solution)/shard_map/ppermute | solution.py:521
  36.1 9.2 %copy-start.7 = (s32[32]{0:T(128)S(1)}, s32[32]{0:T(128)}, u32[]{:S(2)}) copy-start(s32[32]{0:T(128)} %pos_ref.1) | copy-start | bytes 388
  36.1 85.7 %collective-permute-start.2 = (f32[2,128,1024]{2,1,0:T(8,128)}, f32[2,128,1024]{2,1,0:T(8,128)}, u32[]{:S(2)}, u32[]{:S(2)}) collective-permute-start(f32[2,128,1024]{2,1,0:T(8,128)} %get-tuple-element.20), channel_id=1, source_target_pairs={{0,4},{4,0},{1,5},{5,1},{2,6},{6,2},{3,7},{7,3}} | collective-permute-start | bytes 3145736 | tf_op jit(solution)/shard_map/ppermute | solution.py:521
  43.3 78.5 %collective-permute-start = (f32[2,128,1024]{2,1,0:T(8,128)}, f32[2,128,1024]{2,1,0:T(8,128)}, u32[]{:S(2)}, u32[]{:S(2)}) collective-permute-start(f32[2,128,1024]{2,1,0:T(8,128)} %get-tuple-element.18), channel_id=1, source_target_pairs={{0,4},{4,0},{1,5},{5,1},{2,6},{6,2},{3,7},{7,3}} | collective-permute-start | bytes 3145736 | tf_op jit(solution)/shard_map/ppermute | solution.py:521
  46.1 6.9 %copy-start.3 = (bf16[256,2048]{1,0:T(8,128)(2,1)S(1)}, bf16[256,2048]{1,0:T(8,128)(2,1)}, u32[]{:S(2)}) copy-start(bf16[256,2048]{1,0:T(8,128)(2,1)} %front.1.u_ref) | copy-start | bytes 3145732
  46.1 6.9 %copy-start.4 = (bf16[2048,1024]{1,0:T(8,128)(2,1)S(1)}, bf16[2048,1024]{1,0:T(8,128)(2,1)}, u32[]{:S(2)}) copy-start(bf16[2048,1024]{1,0:T(8,128)(2,1)} %param.14) | copy-start | bytes 12582916
  52.3 73.2 %collective-permute-start.1 = (f32[2,128,1024]{2,1,0:T(8,128)}, f32[2,128,1024]{2,1,0:T(8,128)S(1)}, u32[]{:S(2)}, u32[]{:S(2)}) collective-permute-start(f32[2,128,1024]{2,1,0:T(8,128)} %get-tuple-element.19), channel_id=1, source_target_pairs={{0,4},{4,0},{1,5},{5,1},{2,6},{6,2},{3,7},{7,3}} | collective-permute-start | bytes 3145736 | tf_op jit(solution)/shard_map/ppermute | solution.py:521
  55.6 9.4 %all-to-all-start = ((bf16[128,4,256]{2,1,0:T(4,128)(2,1)}), bf16[128,4,256]{2,1,0:T(4,128)(2,1)S(1)}, u32[]{:S(2)}, u32[]{:S(2)}) async-start(bf16[128,4,256]{2,1,0:T(4,128)(2,1)} %reshape.24), calls=%async_computation | async-start | bytes 524288 | tf_op jit(solution)/shard_map/all_to_all | solution.py:527
  125.6 1.1 copy-start.6
  126.6 44.0 %copy-start.1 = (bf16[2048,256]{1,0:T(8,128)(2,1)S(1)}, bf16[2048,256]{1,0:T(8,128)(2,1)}, u32[]{:S(2)}) copy-start(bf16[2048,256]{1,0:T(8,128)(2,1)} %param.15) | copy-start | bytes 3145732
where the time goes:
time: 171 us
  Pallas kernels  128 us (75%)
  starting transfers between devices  9.51 us (6%)
  waiting for transfers between devices  9.14 us (5%)
  blocking collectives  8.39 us (5%)
  local copies, waits for them, and re-layouts  7.31 us (4%)
  matrix products  6.89 us (4%)
    pallas_call x1, Pallas kernels, attention(): pl.pallas_call(functools.partial(attn_kernel, nb, ahead), out_shape=[jax....  45.4 us
    pallas_call x1, Pallas kernels, tail(): pl.pallas_call(functools.partial(tail_kernel, n_gu, cuts, n_w), out_shape...  42.3 us
    pallas_call x4, Pallas kernels, gate_up(): pl.pallas_call(gu_kernel, grid=(cols // blk,), out_shape=[shape, shape],...  25 us
    pallas_call x1, Pallas kernels, front(): pl.pallas_call(functools.partial(front_kernel, nx, ny), out_shape=jax.Sha...  15.1 us
    all_to_all x1, blocking collectives, device_step(): attn_heads = lax.all_to_all(attn_seq, 'tpy', 1, 0, tiled=True)  8.39 us
    dot_general x6, matrix products, dot(): return jnp.dot(a, b, preferred_element_type=F32)  6.89 us
    all_to_all x1, waiting for transfers between devices, device_step(): q_seq = lax.all_to_all(q_heads, 'tpy', 0, 1, tiled=True)  5.36 us
    ppermute x4, starting transfers between devices, device_step(): recv.append(lax.ppermute(s, 'tpx', swap_x))  4.05 us
  transfers between devices with their start and end apart: 7, of which 2 were waited for; matrix products, arithmetic and copies ran while one was open for 4% of the time, Pallas kernels for 41%

commit v1 on v0

v1 whole, which is shorter than its diff:
```python
import functools

import jax
import jax.numpy as jnp
from jax import lax
from jax.experimental import pallas as pl
from jax.experimental.pallas import tpu as pltpu
from jax.sharding import PartitionSpec as P


LN_EPS = 1e-6
ROPE_BASE = 10000.0
MESH = pl.DeviceIdType.MESH
F32 = jnp.float32
BF16 = jnp.bfloat16


def rope_tables(positions, head_dim):
    half_dim = head_dim // 2
    inv_freq = ROPE_BASE ** (-(jnp.arange(half_dim, dtype=F32) * 2.0 / head_dim))
    angles = positions.astype(F32)[:, None] * inv_freq[None, :]
    return jnp.cos(angles), jnp.sin(angles)


def rope(x, cos, sin):
    half = x.shape[-1] // 2
    lead, tail = x[:, :half], x[:, half:]
    return jnp.concatenate([lead * cos - tail * sin, lead * sin + tail * cos], axis=-1)


def front_kernel(nx, ny, ge, gc, h_ref, sc_ref, wq_hbm, wk_hbm, wv_hbm, wg_hbm, wu_hbm,
                 q_ref, kv_ref, ke_ref, re_ref, u_hbm, gs_hbm, gk_hbm,
                 hbuf, scbuf, stat, cols, u_ref, wq, wkv, wgu, qs, qr, qo, kvs, kvr, es, er, gs, gk, qn, qall,
                 wsem, hs, hr, ss, sr, ts, tr, qss, qrs, ls, as_, ar, outs):
    ix, iy = lax.axis_index("tpx"), lax.axis_index("tpy")
    rows, width = h_ref.shape
    n_dev = nx * ny
    half = rows // 2
    n_seq = half // ny
    dim = wk_hbm.shape[1]
    gw = ge + gc
    partner = iy + 1 - 2 * lax.rem(iy, 2)
    cross = lax.rem(iy + 2, ny)
    diag = lax.rem(partner + 2, ny)
    me = ix * ny + iy
    peer_x = {"tpx": 1 - ix, "tpy": iy}

    def remote(src, dst, send, recv, dev):
        return pltpu.make_async_remote_copy(
            src_ref=src, dst_ref=dst, send_sem=send, recv_sem=recv, device_id=dev, device_id_type=MESH
        )

    loads = [
        pltpu.make_async_copy(wq_hbm, wq, wsem.at[0]),
        pltpu.make_async_copy(wk_hbm, wkv.at[0], wsem.at[1]),
        pltpu.make_async_copy(wv_hbm, wkv.at[1], wsem.at[2]),
        pltpu.make_async_copy(wg_hbm.at[:, 0:gw], wgu.at[0], wsem.at[3]),
        pltpu.make_async_copy(wu_hbm.at[:, 0:gw], wgu.at[1], wsem.at[4]),
    ]
    for c in loads:
        c.start()

    others = [(dx, dy) for dx in range(nx) for dy in range(ny) if dx or dy]
    barrier = pltpu.get_barrier_semaphore()
    for dx, dy in others:
        pl.semaphore_signal(
            barrier,
            inc=1,
            device_id={"tpx": lax.rem(ix + dx, nx), "tpy": lax.rem(iy + dy, ny)},
            device_id_type=MESH,
        )
    pl.semaphore_wait(barrier, n_dev - 1)

    n_ch, ch = 4, rows // 4

    def nat(j):
        base = (1 - ix) * half + j * ch if j < n_ch // 2 else ix * half + (j - n_ch // 2) * ch
        return pl.ds(pl.multiple_of(base, ch), ch)

    def perm(j):
        return pl.ds(j * ch, ch)

    def h_copy(j, dst_y, k):
        return remote(h_ref.at[nat(j)], hbuf.at[iy, perm(j)], hs.at[k, j], hr.at[k, j], {"tpx": ix, "tpy": dst_y})

    to_cross = [h_copy(j, cross, 0) for j in range(n_ch)]
    to_partner = [h_copy(j, partner, 1) for j in range(n_ch)]
    to_cross[0].start()
    for c in to_partner:
        c.start()

    hf = h_ref[...].astype(F32)
    total = jnp.sum(hf, axis=1, keepdims=True)
    dev = hf - total / width
    spread = jnp.sum(dev * dev, axis=1, keepdims=True)
    lane = lax.broadcasted_iota(jnp.int32, (rows, 128), 1)
    packed = jnp.where(lane == 0, total, jnp.where(lane == 1, spread, 0.0))
    stat[me] = jnp.transpose(packed)[:2]
    stat_copies = []
    for k, (dx, dy) in enumerate(others):
        c = remote(
            stat.at[me], stat.at[me], ts.at[k], tr.at[k],
            {"tpx": lax.rem(ix + dx, nx), "tpy": lax.rem(iy + dy, ny)},
        )
        c.start()
        stat_copies.append(c)
    sc_copies = []
    for k, dst in enumerate((cross, partner, diag)):
        c = remote(sc_ref, scbuf.at[iy], ss.at[k], sr.at[k], {"tpx": ix, "tpy": dst})
        c.start()
        sc_copies.append(c)
    for c in to_cross[1:]:
        c.start()

    forward = []

    def relay(j):
        to_cross[j].wait_recv()
        part = hbuf.at[cross, perm(j)]
        c = remote(part, part, hs.at[2, j], hr.at[2, j], {"tpx": ix, "tpy": partner})
        c.start()
        forward.append(c)

    relay(0)
    for c in stat_copies:
        c.wait_recv()
    sums = [stat[d, 0:1, :] for d in range(n_dev)]
    sprd = [stat[d, 1:2, :] for d in range(n_dev)]
    mean = functools.reduce(jnp.add, sums) / (width * n_dev)
    m2 = functools.reduce(jnp.add, sprd)
    for d in range(n_dev):
        gap = sums[d] / width - mean
        m2 = m2 + width * gap * gap
    rs = lax.rsqrt(m2 / (width * n_dev) + LN_EPS)
    sub = lax.broadcasted_iota(jnp.int32, (128, rows), 0)
    cols[...] = jnp.transpose(jnp.where(sub == 0, mean, jnp.where(sub == 1, rs, 0.0)))
    for c in sc_copies:
        c.wait_recv()

    def emit(block, scale, owner, j):
        stats = cols[nat(j), :]
        u = ((block.astype(F32) - stats[:, 0:1]) * stats[:, 1:2] * scale).astype(BF16)
        u_ref[perm(j), pl.ds(pl.multiple_of(owner * width, width), width)] = u

    def normalise(j):
        emit(h_ref[nat(j), :], sc_ref[...], iy, j)
        to_partner[j].wait_recv()
        emit(hbuf[partner, perm(j), :], scbuf[partner], partner, j)
        emit(hbuf[cross, perm(j), :], scbuf[cross], cross, j)
        forward[j].wait_recv()
        emit(hbuf[diag, perm(j), :], scbuf[diag], diag, j)

    def dot(a, b):
        return jnp.dot(a, b, preferred_element_type=F32)

    q_copies = []
    for j in range(n_ch):
        if j + 1 < n_ch:
            relay(j + 1)
        normalise(j)
        if j < n_ch // 2:
            if j == 0:
                loads[0].wait()
            qs[perm(j), :] = dot(u_ref[perm(j), :], wq[...])
            c = remote(qs.at[perm(j)], qr.at[perm(j)], qss.at[j], qrs.at[j], peer_x)
            c.start()
            q_copies.append(c)
    loads[1].wait()
    loads[2].wait()
    oth_rows = u_ref[pl.ds(pl.multiple_of(iy * n_seq, n_seq), n_seq), :]
    own_rows = u_ref[pl.ds(pl.multiple_of(half + iy * n_seq, n_seq), n_seq), :]
    for k in range(2):
        kvs[:, k * dim : (k + 1) * dim] = dot(oth_rows, wkv[k])
    kv_copy = remote(kvs, kvr, ls.at[0], ls.at[1], peer_x)
    kv_copy.start()
    u_out = pltpu.make_async_copy(u_ref, u_hbm, outs.at[0])
    u_out.start()
    loads[3].wait()
    loads[4].wait()
    for k in range(2):
        y = dot(u_ref[...], wgu[k, :, 0:ge])
        es[k] = y[:half]
        ke_ref[k] = y[half:]
    e_copy = remote(es, er, ls.at[2], ls.at[3], peer_x)
    e_copy.start()
    qo[...] = dot(u_ref[pl.ds(half, half), :], wq[...])
    own_kv = [dot(own_rows, wkv[k]) for k in range(2)]

    def gate_up_part(lo, hi):
        for k in range(2):
            y = dot(u_ref[...], wgu[k, :, ge + lo : ge + hi])
            gs[k, :, lo:hi] = y[:half]
            gk[k, :, lo:hi] = y[half:]

    gate_up_part(0, gc // 2)
    for j in range(n_ch // 2):
        q_copies[j].wait_recv()
        qn[perm(j), :] = (qo[perm(j), :] + qr[perm(j), :]).astype(BF16)
    q_sends = []
    for k in range(1, ny):
        d = lax.rem(iy + k, ny)
        c = remote(
            qn.at[pl.ds(pl.multiple_of(d * n_seq, n_seq), n_seq)], qall.at[iy],
            as_.at[k - 1], ar.at[k - 1], {"tpx": ix, "tpy": d},
        )
        c.start()
        q_sends.append(c)
    gate_up_part(gc // 2, gc)
    g_out = [pltpu.make_async_copy(gs, gs_hbm, outs.at[1]), pltpu.make_async_copy(gk, gk_hbm, outs.at[2])]
    for c in g_out:
        c.start()
    kv_copy.wait_recv()
    for k in range(2):
        sl = slice(k * dim, (k + 1) * dim)
        kv_ref[:, sl] = (own_kv[k] + kvr[:, sl]).astype(BF16)
    q_ref[iy] = qn[pl.ds(pl.multiple_of(iy * n_seq, n_seq), n_seq), :].astype(F32)
    for k in range(1, ny):
        q_sends[k - 1].wait_recv()
        src = lax.rem(iy + ny - k, ny)
        q_ref[src] = qall[src].astype(F32)
    e_copy.wait_recv()
    re_ref[...] = er[...]
    for c in to_cross + to_partner + forward + sc_copies + stat_copies + q_copies + q_sends + [kv_copy, e_copy]:
        c.wait_send()
    for c in [u_out] + g_out:
        c.wait()


def front(nx, ny, ge, gc, hidden, ln_scale, w_q, w_k, w_v, w_gate, w_up):
    rows, width = hidden.shape
    half = rows // 2
    n_dev, n_seq = nx * ny, rows // (nx * ny)
    kdim, nq = w_q.shape
    dim = w_k.shape[1]
    vm = pl.BlockSpec(memory_space=pltpu.VMEM)
    hbm = pl.BlockSpec(memory_space=pltpu.HBM)
    dma = pltpu.SemaphoreType.DMA
    sds = jax.ShapeDtypeStruct
    return pl.pallas_call(
        functools.partial(front_kernel, nx, ny, ge, gc),
        out_shape=[
            sds((ny, n_seq, nq), F32),
            sds((n_seq, 2 * dim), BF16),
            sds((2, half, ge), F32),
            sds((2, half, ge), F32),
            sds((rows, kdim), BF16),
            sds((2, half, gc), F32),
            sds((2, half, gc), F32),
        ],
        in_specs=[vm, vm] + [hbm] * 5,
        out_specs=[vm] * 4 + [hbm] * 3,
        scratch_shapes=[
            pltpu.VMEM((ny, rows, width), BF16),
            pltpu.VMEM((ny, 1, width), F32),
            pltpu.VMEM((n_dev, 2, rows), F32),
            pltpu.VMEM((rows, 128), F32),
            pltpu.VMEM((rows, kdim), BF16),
            pltpu.VMEM((kdim, nq), BF16),
            pltpu.VMEM((2, kdim, dim), BF16),
            pltpu.VMEM((2, kdim, ge + gc), BF16),
            pltpu.VMEM((half, nq), F32),
            pltpu.VMEM((half, nq), F32),
            pltpu.VMEM((half, nq), F32),
            pltpu.VMEM((n_seq, 2 * dim), F32),
            pltpu.VMEM((n_seq, 2 * dim), F32),
            pltpu.VMEM((2, half, ge), F32),
            pltpu.VMEM((2, half, ge), F32),
            pltpu.VMEM((2, half, gc), F32),
            pltpu.VMEM((2, half, gc), F32),
            pltpu.VMEM((half, nq), BF16),
            pltpu.VMEM((ny, n_seq, nq), BF16),
            dma((5,)),
            dma((3, 4)),
            dma((3, 4)),
            dma((3,)),
            dma((3,)),
            dma((n_dev - 1,)),
            dma((n_dev - 1,)),
            dma((2,)),
            dma((2,)),
            dma((4,)),
            dma((ny - 1,)),
            dma((ny - 1,)),
            dma((3,)),
        ],
        compiler_params=pltpu.CompilerParams(collective_id=0, has_side_effects=True, vmem_limit_bytes=56 * 2**20),
        cost_estimate=pl.CostEstimate(flops=2 * rows * kdim * nq, bytes_accessed=2 * kdim * nq, transcendentals=0),
        name="front",
    )(hidden, ln_scale.reshape(1, width), w_q, w_k, w_v, w_gate, w_up)


def gu_kernel(u_ref, wg_ref, wu_ref, send, keep):
    half = u_ref.shape[0] // 2
    for k, w_ref in enumerate((wg_ref, wu_ref)):
        y = jnp.dot(u_ref[...], w_ref[...], preferred_element_type=F32)
        send[k] = y[:half]
        keep[k] = y[half:]


def gate_up(u, w_gate, w_up, start, cols, blk):
    rows, kdim = u.shape
    half = rows // 2
    first = start // blk
    shape = jax.ShapeDtypeStruct((2, half, cols), F32)
    wspec = pl.BlockSpec((kdim, blk), lambda i: (0, i + first))
    ospec = pl.BlockSpec((2, half, blk), lambda i: (0, 0, i))
    return pl.pallas_call(
        gu_kernel,
        grid=(cols // blk,),
        out_shape=[shape, shape],
        in_specs=[pl.BlockSpec((rows, kdim), lambda i: (0, 0)), wspec, wspec],
        out_specs=[ospec, ospec],
        compiler_params=pltpu.CompilerParams(vmem_limit_bytes=56 * 2**20),
        cost_estimate=pl.CostEstimate(
            flops=4 * rows * kdim * cols, bytes_accessed=4 * kdim * cols, transcendentals=0
        ),
        name="gate_up",
    )(u, w_gate, w_up)


def attn_kernel(nb, ahead, pos_ref, q_ref, kv_ref, cos_ref, sin_ref, kc_ref, vc_ref,
                o_ref, ko_ref, vo_ref, kbuf, vbuf, krow, vrow, qrot, orow, ki, vi, ks, vs):
    n_seq, n_head, dim = qrot.shape
    n_dev = q_ref.shape[0]
    per = n_head // n_dev
    length = kbuf.shape[1]

    def fetch(b, slot):
        pltpu.make_async_copy(kc_ref.at[b], kbuf.at[slot], ki.at[slot]).start()
        pltpu.make_async_copy(vc_ref.at[b], vbuf.at[slot], vi.at[slot]).start()

    def wait_out(b, slot):
        pltpu.make_async_copy(kbuf.at[slot], ko_ref.at[b], ks.at[slot]).wait()
        pltpu.make_async_copy(vbuf.at[slot], vo_ref.at[b], vs.at[slot]).wait()

    for b in range(ahead):
        fetch(b, b)
    krow[...] = rope(kv_ref[:, :dim].astype(F32), cos_ref[...], sin_ref[...]).astype(BF16).astype(F32)
    vrow[...] = kv_ref[:, dim:].astype(F32)
    for d in range(n_dev):
        for h in range(per):
            x = rope(q_ref[d, :, h * dim : (h + 1) * dim], cos_ref[...], sin_ref[...])
            qrot[:, d * per + h, :] = x

    def patch(buf, slot, row, p):
        base = pl.multiple_of((p // 16) * 16, 16)
        old = buf[slot, pl.ds(base, 16), :].astype(F32)
        hit = lax.broadcasted_iota(jnp.int32, old.shape, 0) == p - base
        buf[slot, pl.ds(base, 16), :] = jnp.where(hit, row, old).astype(BF16)

    @pl.loop(0, n_seq // 2)
    def _(i):
        work = []
        for j in range(2):
            b = 2 * i + j
            slot = lax.rem(b, nb)
            nxt = b + ahead
            nslot = lax.rem(nxt, nb)

            @pl.when(jnp.logical_and(nxt < n_seq, nxt >= nb))
            def _():
                wait_out(nxt - nb, nslot)

            @pl.when(nxt < n_seq)
            def _():
                fetch(nxt, nslot)

            work.append((b, slot))
        for b, slot in work:
            p = pos_ref[b]
            pltpu.make_async_copy(kc_ref.at[b], kbuf.at[slot], ki.at[slot]).wait()
            patch(kbuf, slot, krow[pl.ds(b, 1), :], p)
            pltpu.make_async_copy(vc_ref.at[b], vbuf.at[slot], vi.at[slot]).wait()
            patch(vbuf, slot, vrow[pl.ds(b, 1), :], p)
        for b, slot in work:
            p = pos_ref[b]
            q = qrot[b].astype(BF16)
            s = lax.dot_general(q, kbuf[slot], (((1,), (1,)), ((), ())), preferred_element_type=F32)
            s = s * (dim ** -0.5)
            ok = lax.broadcasted_iota(jnp.int32, (n_head, length), 1) <= p
            s = jnp.where(ok, s, -jnp.inf)
            e = jnp.exp(s - jnp.max(s, axis=1, keepdims=True))
            prob = (e / jnp.sum(e, axis=1, keepdims=True)).astype(BF16)
            o = jnp.dot(prob, vbuf[slot], preferred_element_type=F32)
            for h in range(n_head):
                orow[h // per, pl.ds(b, 1), (h % per) * dim : (h % per + 1) * dim] = o[h : h + 1]
        for b, slot in work:
            pltpu.make_async_copy(kbuf.at[slot], ko_ref.at[b], ks.at[slot]).start()
            pltpu.make_async_copy(vbuf.at[slot], vo_ref.at[b], vs.at[slot]).start()

    o_ref[...] = orow[...].astype(BF16)
    for b in range(n_seq - nb, n_seq):
        wait_out(b, b % nb)


def attention(q, kv_new, cos, sin, k_cache, v_cache, positions, nb=8, ahead=4):
    n_seq, length, dim = k_cache.shape
    n_head = q.shape[0] * q.shape[2] // dim
    vm = pl.BlockSpec(memory_space=pltpu.VMEM)
    hbm = pl.BlockSpec(memory_space=pltpu.HBM)
    return pl.pallas_call(
        functools.partial(attn_kernel, nb, ahead),
        out_shape=[
            jax.ShapeDtypeStruct(q.shape, BF16),
            jax.ShapeDtypeStruct(k_cache.shape, BF16),
            jax.ShapeDtypeStruct(v_cache.shape, BF16),
        ],
        in_specs=[pl.BlockSpec(memory_space=pltpu.SMEM), vm, vm, vm, vm, hbm, hbm],
        out_specs=[vm, hbm, hbm],
        scratch_shapes=[
            pltpu.VMEM((nb, length, dim), BF16),
            pltpu.VMEM((nb, length, dim), BF16),
            pltpu.VMEM((n_seq, dim), F32),
            pltpu.VMEM((n_seq, dim), F32),
            pltpu.VMEM((n_seq, n_head, dim), F32),
            pltpu.VMEM(q.shape, F32),
            pltpu.SemaphoreType.DMA((nb,)),
            pltpu.SemaphoreType.DMA((nb,)),
            pltpu.SemaphoreType.DMA((nb,)),
            pltpu.SemaphoreType.DMA((nb,)),
        ],
        compiler_params=pltpu.CompilerParams(vmem_limit_bytes=56 * 2**20),
        cost_estimate=pl.CostEstimate(
            flops=4 * 10**10, bytes_accessed=8 * n_seq * length * dim, transcendentals=n_seq * n_head * length
        ),
        name="attention",
    )(positions, q, kv_new, cos, sin, k_cache, v_cache)


def tail_kernel(n_gu, cuts, n_w, *refs):
    keeps, recvs = refs[:n_gu], refs[n_gu : 2 * n_gu]
    (o_ref, h_ref, wd_hbm, wo_hbm, out_ref, wd, kbuf, rbuf, aown, aoth, give, hold, got1, pass_, got2,
     wsem, ksem, rsem, as_, ar, s1, r1, s2, r2, os_, or_) = refs[2 * n_gu :]
    ix, iy = lax.axis_index("tpx"), lax.axis_index("tpy")
    half = aown.shape[0]
    ny, n_seq = o_ref.shape[0], o_ref.shape[1]
    starts, at = [], 0
    for ref in keeps:
        starts.append((at, ref.shape[2]))
        at += ref.shape[2]
    width = h_ref.shape[1]
    kact, ko = wd_hbm.shape[0], wo_hbm.shape[0]
    partner = iy + 1 - 2 * lax.rem(iy, 2)
    cross = lax.rem(iy + 2, 4)
    core, chip = lax.rem(iy, 2), iy // 2
    peer_x = {"tpx": 1 - ix, "tpy": iy}
    peer_core = {"tpx": ix, "tpy": partner}
    peer_chip = {"tpx": ix, "tpy": cross}

    gu_loads = []
    for r, (r0, rn) in enumerate(cuts):
        group = []
        rows = pl.ds(r0, rn)
        for g in range(n_gu):
            part = pl.ds(*starts[g])
            group.append(pltpu.make_async_copy(keeps[g].at[:, rows], kbuf.at[:, rows, part], ksem.at[r, g]))
            group.append(pltpu.make_async_copy(recvs[g].at[:, rows], rbuf.at[:, rows, part], rsem.at[r, g]))
        for c in group:
            c.start()
        gu_loads.append(group)
    step = kact // n_w
    w_loads = []
    for j in range(n_w + 1):
        if j < n_w:
            src, dst = wd_hbm.at[pl.ds(j * step, step)], wd.at[pl.ds(j * step, step)]
        else:
            src, dst = wo_hbm, wd.at[pl.ds(kact, ko)]
        c = pltpu.make_async_copy(src, dst, wsem.at[j])
        c.start()
        w_loads.append(c)

    barrier = pltpu.get_barrier_semaphore()
    others = [(dx, dy) for dx in (1, 0) for dy in range(ny) if dx or dy]

    def shifted(dx, dy):
        return {"tpx": lax.rem(ix + dx, 2), "tpy": lax.rem(iy + dy, ny)}

    for dx, dy in others:
        pl.semaphore_signal(barrier, inc=1, device_id=shifted(dx, dy), device_id_type=MESH)
    pl.semaphore_wait(barrier, len(others))

    o_rows = pl.ds(pl.multiple_of(iy * n_seq, n_seq), n_seq)
    o_cols = pl.ds(kact, ko)
    o_copies = []
    for k, (dx, dy) in enumerate(others):
        c = pltpu.make_async_remote_copy(
            src_ref=o_ref.at[lax.rem(iy + dy, ny)],
            dst_ref=(aoth if dx else aown).at[o_rows, o_cols],
            send_sem=os_.at[k],
            recv_sem=or_.at[k],
            device_id=shifted(dx, dy),
            device_id_type=MESH,
        )
        c.start()
        o_copies.append(c)
    aown[o_rows, kact:] = o_ref[iy]

    sends = []
    for r, (r0, rn) in enumerate(cuts):
        rows = pl.ds(r0, rn)
        for c in gu_loads[r]:
            c.wait()
        for g in range(n_gu):
            part = pl.ds(*starts[g])
            gate = (kbuf[0, rows, part] + rbuf[0, rows, part]).astype(BF16).astype(F32)
            up = (kbuf[1, rows, part] + rbuf[1, rows, part]).astype(BF16).astype(F32)
            aown[rows, part] = (jax.nn.silu(gate) * up).astype(BF16)
        c = pltpu.make_async_remote_copy(
            src_ref=aown.at[rows, pl.ds(0, kact)],
            dst_ref=aoth.at[rows, pl.ds(0, kact)],
            send_sem=as_.at[r],
            recv_sem=ar.at[r],
            device_id=peer_x,
            device_id_type=MESH,
        )
        c.start()
        sends.append(c)
    for c in w_loads:
        c.wait()
    for c in o_copies:
        c.wait_recv()

    blocks = [(half, half)] + [(r0, rn) for r0, rn in cuts]

    def product(lhs, x, c):
        col = pl.ds(pl.multiple_of((x * 2 + c) * width, width), width)
        return jnp.dot(lhs, wd[:, col], preferred_element_type=F32)

    stage1, stage2 = [], []

    def run_block(k):
        r0, rn = blocks[k]
        rows = pl.ds(r0, rn)
        if k == 0:
            lhs = aown[...]
        else:
            sends[k - 1].wait_recv()
            lhs = aoth[rows, :]
        for x in range(2):
            give[x, rows, :] = product(lhs, x, 1 - core)
        c = pltpu.make_async_remote_copy(
            src_ref=give.at[:, rows],
            dst_ref=got1.at[:, rows],
            send_sem=s1.at[k],
            recv_sem=r1.at[k],
            device_id=peer_core,
            device_id_type=MESH,
        )
        c.start()
        stage1.append(c)
        hold[0, rows, :] = product(lhs, 1 - chip, core)
        hold[1, rows, :] = product(lhs, chip, core)

    def reduce_block(k):
        r0, rn = blocks[k]
        rows = pl.ds(r0, rn)
        stage1[k].wait_recv()
        pass_[rows, :] = hold[0, rows, :] + got1[1 - chip, rows, :]
        c = pltpu.make_async_remote_copy(
            src_ref=pass_.at[rows],
            dst_ref=got2.at[rows],
            send_sem=s2.at[k],
            recv_sem=r2.at[k],
            device_id=peer_chip,
            device_id_type=MESH,
        )
        c.start()
        stage2.append(c)

    def finish_block(k):
        r0, rn = blocks[k]
        rows = pl.ds(r0, rn)
        stage2[k].wait_recv()
        total = hold[1, rows, :] + got1[chip, rows, :] + got2[rows, :]
        base = ix * half if k == 0 else (1 - ix) * half + r0
        nat = pl.ds(pl.multiple_of(base, 32), rn)
        out_ref[nat, :] = (h_ref[nat, :].astype(F32) + total).astype(BF16)

    n_blk = len(blocks)
    for k in range(n_blk):
        run_block(k)
        if k:
            reduce_block(k - 1)
    reduce_block(n_blk - 1)
    for k in range(n_blk):
        finish_block(k)
    for c in sends + stage1 + stage2 + o_copies:
        c.wait_send()


def tail(keeps, recvs, o, hidden, w_down, w_o):
    rows, width = hidden.shape
    n_gu = len(keeps)
    half = keeps[0].shape[1]
    n = w_down.shape[1]
    kdim = w_down.shape[0] + w_o.shape[0]
    cuts = [(0, 64), (64, 32), (96, 32)]
    n_w, n_cut, n_blk = 8, len(cuts), len(cuts) + 1
    vm = pl.BlockSpec(memory_space=pltpu.VMEM)
    anywhere = pl.BlockSpec(memory_space=pl.ANY)
    dma = pltpu.SemaphoreType.DMA
    return pl.pallas_call(
        functools.partial(tail_kernel, n_gu, cuts, n_w),
        out_shape=jax.ShapeDtypeStruct((rows, width), BF16),
        in_specs=[anywhere] * (2 * n_gu) + [vm, vm] + [pl.BlockSpec(memory_space=pltpu.HBM)] * 2,
        out_specs=vm,
        scratch_shapes=[
            pltpu.VMEM((kdim, n), BF16),
            pltpu.VMEM((2, half, w_down.shape[0]), F32),
            pltpu.VMEM((2, half, w_down.shape[0]), F32),
            pltpu.VMEM((half, kdim), BF16),
            pltpu.VMEM((half, kdim), BF16),
            pltpu.VMEM((2, rows, width), F32),
            pltpu.VMEM((2, rows, width), F32),
            pltpu.VMEM((2, rows, width), F32),
            pltpu.VMEM((rows, width), F32),
            pltpu.VMEM((rows, width), F32),
            dma((n_w + 1,)),
            dma((n_cut, n_gu)),
            dma((n_cut, n_gu)),
            dma((n_cut,)),
            dma((n_cut,)),
            dma((n_blk,)),
            dma((n_blk,)),
            dma((n_blk,)),
            dma((n_blk,)),
            dma((7,)),
            dma((7,)),
        ],
        compiler_params=pltpu.CompilerParams(collective_id=1, has_side_effects=True, vmem_limit_bytes=56 * 2**20),
        cost_estimate=pl.CostEstimate(flops=2 * rows * kdim * n, bytes_accessed=2 * kdim * n, transcendentals=0),
        name="tail",
    )(*keeps, *recvs, o, hidden, w_down, w_o)


def solution(mesh):
    x_size = mesh.shape["tpx"]
    y_size = mesh.shape["tpy"]
    hidden_spec = P("dp", ("tpx", "tpy"))
    cache_spec = P(("dp", "tpx", "tpy"), None, None)
    in_specs = (hidden_spec, P(("tpx", "tpy")), P("tpx", "tpy"), P("tpx", None), P("tpx", None), P("tpx", "tpy"), P("tpx", "tpy"), P("tpy", "tpx"), P("tpy", "tpx"), cache_spec, cache_spec, P(("dp", "tpx", "tpy")))
    out_specs = (hidden_spec, cache_spec, cache_spec)
    swap_x = [(0, 1), (1, 0)]
    ge, sizes = 256, (1024, 1024, 1024, 768)

    def device_step(hidden, ln_scale, w_q, w_k, w_v, w_gate, w_up, w_o, w_down, k_cache, v_cache, positions):
        q, kv_new, keep_e, recv_e, u, send, keep_0 = front(
            x_size, y_size, ge, sizes[0], hidden, ln_scale, w_q, w_k, w_v, w_gate, w_up
        )
        keep, recv = [keep_e, keep_0], [recv_e]
        at = ge + sizes[0]
        for c, n in enumerate(sizes):
            if c:
                send, k = gate_up(u, w_gate, w_up, at, n, 256)
                keep.append(k)
                at += n
            recv.append(lax.ppermute(send, "tpx", swap_x))

        cos_tab, sin_tab = rope_tables(positions, k_cache.shape[2])
        o, k_all, v_all = attention(q, kv_new, cos_tab, sin_tab, k_cache, v_cache, positions)
        hidden_out = tail(keep, recv, o, hidden, w_down, w_o)
        return hidden_out, k_all, v_all

    return jax.shard_map(device_step, mesh=mesh, in_specs=in_specs, out_specs=out_specs, check_vma=False)
```

time: 171 us -> 164 us (0.959)
  Pallas kernels: 128 us -> 139 us
  blocking collectives: 8.39 us -> 0 us
  waiting for transfers between devices: 9.14 us -> 16.4 us
  matrix products: 6.89 us -> 0 us
  starting transfers between devices: 9.51 us -> 4.07 us
  local copies, waits for them, and re-layouts: 7.31 us -> 2.69 us
    pallas_call x1, Pallas kernels: 15.1 us -> 32.5 us  [front(): pl.pallas_call(functools.partial(front_kernel, nx, ny, ge, gc), out_shape...]
    ppermute x6 -> x4, waiting for transfers between devices: 3.78 us -> 16.4 us  [device_step(): recv.append(lax.ppermute(send, 'tpx', swap_x))]
    all_to_all x1 -> x0, blocking collectives: 8.39 us -> none  [device_step(): attn_heads = lax.all_to_all(attn_seq, 'tpy', 1, 0, tiled=True)]
    dot_general x6 -> x0, matrix products: 6.89 us -> none  [dot(): return jnp.dot(a, b, preferred_element_type=F32)]
    all_to_all x1 -> x0, waiting for transfers between devices: 5.36 us -> none  [device_step(): q_seq = lax.all_to_all(q_heads, 'tpy', 0, 1, tiled=True)]
    pallas_call x4 -> x3, Pallas kernels: 25 us -> 19.7 us  [gate_up(): pl.pallas_call(gu_kernel, grid=(cols // blk,), out_shape=[shape, shape],...]
    all_to_all x1 -> x0, starting transfers between devices: 3.41 us -> none  [device_step(): q_seq = lax.all_to_all(q_heads, 'tpy', 0, 1, tiled=True)]
    ppermute x6 -> x4, starting transfers between devices: 6.1 us -> 4.07 us  [device_step(): recv.append(lax.ppermute(send, 'tpx', swap_x))]
  transfers between devices with their start and end apart: 7 -> 4, of which waited for: 2 -> 1; matrix products, arithmetic and copies ran while one was open for 4% -> 0% of each run, Pallas kernels for 41% -> 40%
where the time goes in v1:
time: 164 us
  Pallas kernels  139 us (85%)
  waiting for transfers between devices  16.4 us (10%)
  starting transfers between devices  4.07 us (2%)
  local copies, waits for them, and re-layouts  2.69 us (2%)
    pallas_call x1, Pallas kernels, attention(): pl.pallas_call(functools.partial(attn_kernel, nb, ahead), out_shape=[jax....  45.2 us
    pallas_call x1, Pallas kernels, tail(): pl.pallas_call(functools.partial(tail_kernel, n_gu, cuts, n_w), out_shape...  42.1 us
    pallas_call x1, Pallas kernels, front(): pl.pallas_call(functools.partial(front_kernel, nx, ny, ge, gc), out_shape...  32.5 us
    pallas_call x3, Pallas kernels, gate_up(): pl.pallas_call(gu_kernel, grid=(cols // blk,), out_shape=[shape, shape],...  19.7 us
    ppermute x4, waiting for transfers between devices, device_step(): recv.append(lax.ppermute(send, 'tpx', swap_x))  16.4 us
    ppermute x4, starting transfers between devices, device_step(): recv.append(lax.ppermute(send, 'tpx', swap_x))  4.07 us
  transfers between devices with their start and end apart: 4, of which 1 were waited for; matrix products, arithmetic and copies ran while one was open for 0% of the time, Pallas kernels for 40%

profile of v1, /device:TPU:0, one launch (start us, length us, event | category | flops | bytes accessed | tf_op | source)
XLA Modules:
  0.0 164.1 jit_solution(17019890658580318286)
XLA Ops:
  0.6 32.5 %front.1 = (f32[4,32,1024]{2,1,0:T(8,128)}, bf16[32,512]{1,0:T(8,128)(2,1)}, f32[2,128,256]{2,1,0:T(8,128)}, f32[2,128,256]{2,1,0:T(8,128)}, bf16[256,2048]{1,0:...) custom-call(bf16[256,512]{1,0:T(8,128)(2,1)} %refs_11_.1, f32[1,512]{1,0:T(1,128)} %bitcast.1, ...), custom_call_target="tpu_custom_call" | custom-call | flops 1073741824 | bytes 4194304 | tf_op jit(solution)/shard_map/front/pallas_call | solution.py:239
  33.1 1.2 collective-permute-start
  34.3 6.1 %gate_up.5 = (f32[2,128,768]{2,1,0:T(8,128)}, f32[2,128,768]{2,1,0:T(8,128)}) custom-call(bf16[256,2048]{1,0:T(8,128)(2,1)} %get-tuple-element.21.u_ref, bf16[2048,4096]{1,0:T(8,128)(2,1)} %wg_ref.5, bf16[2048,4096]{1,0:T(8,128)(2,1)} %wu_ref.5), custom_call_target="tpu_custom_call" | custom-call | flops 1610612736 | bytes 6291456 | tf_op jit(solution)/shard_map/gate_up/pallas_call | solution.py:307
  40.4 0.8 collective-permute-start.3
  41.2 6.8 %gate_up.3 = (f32[2,128,1024]{2,1,0:T(8,128)}, f32[2,128,1024]{2,1,0:T(8,128)}) custom-call(bf16[256,2048]{1,0:T(8,128)(2,1)} %get-tuple-element.21.u_ref, bf16[2048,4096]{1,0:T(8,128)(2,1)} %wg_ref.5, bf16[2048,4096]{1,0:T(8,128)(2,1)} %wu_ref.5), custom_call_target="tpu_custom_call" | custom-call | flops 2147483648 | bytes 8388608 | tf_op jit(solution)/shard_map/gate_up/pallas_call | solution.py:307
  48.1 0.0 copy-start.4
  48.1 1.2 collective-permute-start.1
  49.3 6.8 %gate_up.4 = (f32[2,128,1024]{2,1,0:T(8,128)}, f32[2,128,1024]{2,1,0:T(8,128)}) custom-call(bf16[256,2048]{1,0:T(8,128)(2,1)} %get-tuple-element.21.u_ref, bf16[2048,4096]{1,0:T(8,128)(2,1)} %wg_ref.5, bf16[2048,4096]{1,0:T(8,128)(2,1)} %wu_ref.5), custom_call_target="tpu_custom_call" | custom-call | flops 2147483648 | bytes 8388608 | tf_op jit(solution)/shard_map/gate_up/pallas_call | solution.py:307
  56.1 0.8 collective-permute-start.2
  56.9 0.0 copy-done.4
  57.0 0.8 multiply_sine_fusion
  57.7 45.2 %attention.1 = (bf16[4,32,1024]{2,1,0:T(8,128)(2,1)}, bf16[32,2048,256]{2,1,0:T(8,128)(2,1)}, bf16[32,2048,256]{2,1,0:T(8,128)(2,1)}) custom-call(s32[32]{0:T(128)} %pos_ref.1, f32[4,32,1024]{2,1,0:T(8,128)} %get-tuple-element.30.q_ref, bf16[32,512]{1,0:T(8,128)(2,1)} %get-tuple-element.31.kv_ref, f32[32,128]{1,0:T(8,128)} %get-tuple-element.36.cos_ref, ...), custom_call_target="tpu_custom_call" | custom-call | flops 40000000000 | bytes 134217728 | tf_op jit(solution)/shard_map/attention/pallas_call | solution.py:401
  102.9 0.0 collective-permute-done.3.refs_9_
  102.9 0.0 copy-start.3
  102.9 0.0 collective-permute-done.refs_6_
  102.9 0.0 copy-start
  102.9 0.0 collective-permute-done.1.refs_7_
  102.9 0.0 copy-start.1
  102.9 16.4 %collective-permute-done.2.refs_8_ = f32[2,128,1024]{2,1,0:T(8,128)S(1)} collective-permute-done((f32[2,128,1024]{2,1,0:T(8,128)}, f32[2,128,1024]{2,1,0:T(8,128)S(1)}, u32[]{:S(2)}, u32[]{:S(2)}) %collective-permute-start.2) | collective-permute-done | bytes 1048608 | tf_op jit(solution)/shard_map/ppermute | solution.py:657
  119.3 0.0 copy-start.2
  119.3 0.0 copy-done.3
  119.3 0.0 copy-done
  119.3 0.0 copy-done.1
  119.3 1.0 copy-done.2
  120.3 42.1 %tail.1 = bf16[256,512]{1,0:T(8,128)(2,1)} custom-call(f32[2,128,256]{2,1,0:T(8,128)} %get-tuple-element.19.refs_0_, f32[2,128,1024]{2,1,0:T(8,128)} %get-tuple-element.20.refs_1_, f32[2,128,1024]{2,1,0:T(8,128)} %get-tuple-element.22.refs_2_, f32[2,128,1024]{2,1,0:T(8,128)} %get-tuple-element.23.refs_3_, f32[2,128,768]{2,1,0:T(8,128)} %get-tuple-element.24.refs_4_, ...), custom_call_target="tpu_custom_call" | custom-call | flops 5368709120 | bytes 20971520 | tf_op jit(solution)/shard_map/tail/pallas_call | solution.py:602
  162.5 1.7 %copy.16 = bf16[256,512]{1,0:T(8,128)(2,1)} copy(bf16[256,512]{1,0:T(8,128)(2,1)} %tail.1) | data formatting | bytes 524288
  (2 shorter events, 0.0 us)
Async XLA Ops:
  33.1 69.8 %collective-permute-start = (f32[2,128,1024]{2,1,0:T(8,128)}, f32[2,128,1024]{2,1,0:T(8,128)S(1)}, u32[]{:S(2)}, u32[]{:S(2)}) collective-permute-start(f32[2,128,1024]{2,1,0:T(8,128)} %get-tuple-element.26), channel_id=1, source_target_pairs={{0,4},{4,0},{1,5},{5,1},{2,6},{6,2},{3,7},{7,3}} | collective-permute-start | bytes 3145736 | tf_op jit(solution)/shard_map/ppermute | solution.py:657
  40.4 62.5 %collective-permute-start.3 = (f32[2,128,768]{2,1,0:T(8,128)}, f32[2,128,768]{2,1,0:T(8,128)S(1)}, u32[]{:S(2)}, u32[]{:S(2)}) collective-permute-start(f32[2,128,768]{2,1,0:T(8,128)} %get-tuple-element.29), channel_id=1, source_target_pairs={{0,4},{4,0},{1,5},{5,1},{2,6},{6,2},{3,7},{7,3}} | collective-permute-start | bytes 2359304 | tf_op jit(solution)/shard_map/ppermute | solution.py:657
  48.1 8.9 %copy-start.4 = (s32[32]{0:T(128)S(1)}, s32[32]{0:T(128)}, u32[]{:S(2)}) copy-start(s32[32]{0:T(128)} %pos_ref.1) | copy-start | bytes 388
  48.1 54.8 %collective-permute-start.1 = (f32[2,128,1024]{2,1,0:T(8,128)}, f32[2,128,1024]{2,1,0:T(8,128)S(1)}, u32[]{:S(2)}, u32[]{:S(2)}) collective-permute-start(f32[2,128,1024]{2,1,0:T(8,128)} %get-tuple-element.27), channel_id=1, source_target_pairs={{0,4},{4,0},{1,5},{5,1},{2,6},{6,2},{3,7},{7,3}} | collective-permute-start | bytes 3145736 | tf_op jit(solution)/shard_map/ppermute | solution.py:657
  56.1 63.2 %collective-permute-start.2 = (f32[2,128,1024]{2,1,0:T(8,128)}, f32[2,128,1024]{2,1,0:T(8,128)S(1)}, u32[]{:S(2)}, u32[]{:S(2)}) collective-permute-start(f32[2,128,1024]{2,1,0:T(8,128)} %get-tuple-element.28), channel_id=1, source_target_pairs={{0,4},{4,0},{1,5},{5,1},{2,6},{6,2},{3,7},{7,3}} | collective-permute-start | bytes 3145736 | tf_op jit(solution)/shard_map/ppermute | solution.py:657
  102.9 16.4 %copy-start.3 = (f32[2,128,768]{2,1,0:T(8,128)}, f32[2,128,768]{2,1,0:T(8,128)S(1)}, u32[]{:S(2)}) copy-start(f32[2,128,768]{2,1,0:T(8,128)S(1)} %collective-permute-done.3.refs_9_) | copy-start | bytes 2359300
  102.9 16.4 %copy-start = (f32[2,128,1024]{2,1,0:T(8,128)}, f32[2,128,1024]{2,1,0:T(8,128)S(1)}, u32[]{:S(2)}) copy-start(f32[2,128,1024]{2,1,0:T(8,128)S(1)} %collective-permute-done.refs_6_) | copy-start | bytes 3145732
  102.9 16.4 %copy-start.1 = (f32[2,128,1024]{2,1,0:T(8,128)}, f32[2,128,1024]{2,1,0:T(8,128)S(1)}, u32[]{:S(2)}) copy-start(f32[2,128,1024]{2,1,0:T(8,128)S(1)} %collective-permute-done.1.refs_7_) | copy-start | bytes 3145732
  119.3 1.0 copy-start.2

commit v2 on v1

--- a/solution.py
+++ b/solution.py
@@ -29,8 +29,8 @@
 
 
 def front_kernel(nx, ny, ge, gc, h_ref, sc_ref, wq_hbm, wk_hbm, wv_hbm, wg_hbm, wu_hbm,
-                 q_ref, kv_ref, ke_ref, re_ref, u_hbm, gs_hbm, gk_hbm,
-                 hbuf, scbuf, stat, cols, u_ref, wq, wkv, wgu, qs, qr, qo, kvs, kvr, es, er, gs, gk, qn, qall,
+                 q_hbm, kv_hbm, ke_hbm, re_hbm, u_hbm, gs_hbm, gk_hbm,
+                 hbuf, scbuf, stat, cols, u_ref, wq, wkv, wgu, qs, qr, qo, kvs, kvr, es, er, ke, gs, gk, qn, qall, qf, kvn,
                  wsem, hs, hr, ss, sr, ts, tr, qss, qrs, ls, as_, ar, outs):
     ix, iy = lax.axis_index("tpx"), lax.axis_index("tpy")
     rows, width = h_ref.shape
@@ -71,14 +71,16 @@
         )
     pl.semaphore_wait(barrier, n_dev - 1)
 
-    n_ch, ch = 4, rows // 4
+    chunks = [(0, 32), (32, half - 32), (half, half // 2), (half + half // 2, half // 2)]
+    n_ch = len(chunks)
 
     def nat(j):
-        base = (1 - ix) * half + j * ch if j < n_ch // 2 else ix * half + (j - n_ch // 2) * ch
-        return pl.ds(pl.multiple_of(base, ch), ch)
+        r0, rn = chunks[j]
+        base = (1 - ix) * half + r0 if r0 < half else ix * half + r0 - half
+        return pl.ds(pl.multiple_of(base, 32), rn)
 
     def perm(j):
-        return pl.ds(j * ch, ch)
+        return pl.ds(*chunks[j])
 
     def h_copy(j, dst_y, k):
         return remote(h_ref.at[nat(j)], hbuf.at[iy, perm(j)], hs.at[k, j], hr.at[k, j], {"tpx": ix, "tpy": dst_y})
@@ -155,7 +157,7 @@
 
     q_copies = []
     for j in range(n_ch):
-        if j + 1 < n_ch:
+        if 0 < j < n_ch - 1:
             relay(j + 1)
         normalise(j)
         if j < n_ch // 2:
@@ -165,6 +167,8 @@
             c = remote(qs.at[perm(j)], qr.at[perm(j)], qss.at[j], qrs.at[j], peer_x)
             c.start()
             q_copies.append(c)
+        if j == 0:
+            relay(1)
     loads[1].wait()
     loads[2].wait()
     oth_rows = u_ref[pl.ds(pl.multiple_of(iy * n_seq, n_seq), n_seq), :]
@@ -180,9 +184,11 @@
     for k in range(2):
         y = dot(u_ref[...], wgu[k, :, 0:ge])
         es[k] = y[:half]
-        ke_ref[k] = y[half:]
+        ke[k] = y[half:]
     e_copy = remote(es, er, ls.at[2], ls.at[3], peer_x)
     e_copy.start()
+    ke_out = pltpu.make_async_copy(ke, ke_hbm, outs.at[3])
+    ke_out.start()
     qo[...] = dot(u_ref[pl.ds(half, half), :], wq[...])
     own_kv = [dot(own_rows, wkv[k]) for k in range(2)]
 
@@ -212,17 +218,22 @@
     kv_copy.wait_recv()
     for k in range(2):
         sl = slice(k * dim, (k + 1) * dim)
-        kv_ref[:, sl] = (own_kv[k] + kvr[:, sl]).astype(BF16)
-    q_ref[iy] = qn[pl.ds(pl.multiple_of(iy * n_seq, n_seq), n_seq), :].astype(F32)
+        kvn[:, sl] = (own_kv[k] + kvr[:, sl]).astype(BF16)
+    kv_out = pltpu.make_async_copy(kvn, kv_hbm, outs.at[4])
+    kv_out.start()
+    qf[iy] = qn[pl.ds(pl.multiple_of(iy * n_seq, n_seq), n_seq), :].astype(F32)
     for k in range(1, ny):
         q_sends[k - 1].wait_recv()
         src = lax.rem(iy + ny - k, ny)
-        q_ref[src] = qall[src].astype(F32)
+        qf[src] = qall[src].astype(F32)
+    q_out = pltpu.make_async_copy(qf, q_hbm, outs.at[5])
+    q_out.start()
     e_copy.wait_recv()
-    re_ref[...] = er[...]
+    re_out = pltpu.make_async_copy(er, re_hbm, outs.at[6])
+    re_out.start()
     for c in to_cross + to_partner + forward + sc_copies + stat_copies + q_copies + q_sends + [kv_copy, e_copy]:
         c.wait_send()
-    for c in [u_out] + g_out:
+    for c in [u_out, ke_out, kv_out, q_out, re_out] + g_out:
         c.wait()
 
 
@@ -248,7 +259,7 @@
             sds((2, half, gc), F32),
         ],
         in_specs=[vm, vm] + [hbm] * 5,
-        out_specs=[vm] * 4 + [hbm] * 3,
+        out_specs=[hbm] * 7,
         scratch_shapes=[
             pltpu.VMEM((ny, rows, width), BF16),
             pltpu.VMEM((ny, 1, width), F32),
@@ -265,10 +276,13 @@
             pltpu.VMEM((n_seq, 2 * dim), F32),
             pltpu.VMEM((2, half, ge), F32),
             pltpu.VMEM((2, half, ge), F32),
+            pltpu.VMEM((2, half, ge), F32),
             pltpu.VMEM((2, half, gc), F32),
             pltpu.VMEM((2, half, gc), F32),
             pltpu.VMEM((half, nq), BF16),
             pltpu.VMEM((ny, n_seq, nq), BF16),
+            pltpu.VMEM((ny, n_seq, nq), F32),
+            pltpu.VMEM((n_seq, 2 * dim), BF16),
             dma((5,)),
             dma((3, 4)),
             dma((3, 4)),
@@ -281,7 +295,7 @@
             dma((4,)),
             dma((ny - 1,)),
             dma((ny - 1,)),
-            dma((3,)),
+            dma((7,)),
         ],
         compiler_params=pltpu.CompilerParams(collective_id=0, has_side_effects=True, vmem_limit_bytes=56 * 2**20),
         cost_estimate=pl.CostEstimate(flops=2 * rows * kdim * nq, bytes_accessed=2 * kdim * nq, transcendentals=0),
@@ -419,7 +433,7 @@
             pltpu.SemaphoreType.DMA((nb,)),
             pltpu.SemaphoreType.DMA((nb,)),
         ],
-        compiler_params=pltpu.CompilerParams(vmem_limit_bytes=56 * 2**20),
+        compiler_params=pltpu.CompilerParams(vmem_limit_bytes=40 * 2**20),
         cost_estimate=pl.CostEstimate(
             flops=4 * 10**10, bytes_accessed=8 * n_seq * length * dim, transcendentals=n_seq * n_head * length
         ),
@@ -429,7 +443,7 @@
 
 def tail_kernel(n_gu, cuts, n_w, *refs):
     keeps, recvs = refs[:n_gu], refs[n_gu : 2 * n_gu]
-    (o_ref, h_ref, wd_hbm, wo_hbm, out_ref, wd, kbuf, rbuf, aown, aoth, give, hold, got1, pass_, got2,
+    (o_ref, wd_hbm, wo_hbm, out_ref, wd, kbuf, rbuf, aown, aoth, give, hold, got1, pass_, got2,
      wsem, ksem, rsem, as_, ar, s1, r1, s2, r2, os_, or_) = refs[2 * n_gu :]
     ix, iy = lax.axis_index("tpx"), lax.axis_index("tpy")
     half = aown.shape[0]
@@ -438,7 +452,7 @@
     for ref in keeps:
         starts.append((at, ref.shape[2]))
         at += ref.shape[2]
-    width = h_ref.shape[1]
+    width = out_ref.shape[1]
     kact, ko = wd_hbm.shape[0], wo_hbm.shape[0]
     partner = iy + 1 - 2 * lax.rem(iy, 2)
     cross = lax.rem(iy + 2, 4)
@@ -528,33 +542,23 @@
 
     stage1, stage2 = [], []
 
-    def run_block(k):
-        r0, rn = blocks[k]
-        rows = pl.ds(r0, rn)
-        if k == 0:
-            lhs = aown[...]
-        else:
-            sends[k - 1].wait_recv()
-            lhs = aoth[rows, :]
-        for x in range(2):
-            give[x, rows, :] = product(lhs, x, 1 - core)
+    def give_block(k, rows, lhs, x):
+        give[x, rows, :] = product(lhs, x, 1 - core)
         c = pltpu.make_async_remote_copy(
-            src_ref=give.at[:, rows],
-            dst_ref=got1.at[:, rows],
-            send_sem=s1.at[k],
-            recv_sem=r1.at[k],
+            src_ref=give.at[x, rows],
+            dst_ref=got1.at[x, rows],
+            send_sem=s1.at[k, len(stage1[k])],
+            recv_sem=r1.at[k, len(stage1[k])],
             device_id=peer_core,
             device_id_type=MESH,
         )
         c.start()
-        stage1.append(c)
-        hold[0, rows, :] = product(lhs, 1 - chip, core)
-        hold[1, rows, :] = product(lhs, chip, core)
+        stage1[k].append(c)
 
     def reduce_block(k):
         r0, rn = blocks[k]
         rows = pl.ds(r0, rn)
-        stage1[k].wait_recv()
+        stage1[k][0].wait_recv()
         pass_[rows, :] = hold[0, rows, :] + got1[1 - chip, rows, :]
         c = pltpu.make_async_remote_copy(
             src_ref=pass_.at[rows],
@@ -567,42 +571,56 @@
         c.start()
         stage2.append(c)
 
+    def run_block(k, last):
+        r0, rn = blocks[k]
+        rows = pl.ds(r0, rn)
+        stage1.append([])
+        if k == 0:
+            lhs = aown[...]
+        else:
+            sends[k - 1].wait_recv()
+            lhs = aoth[rows, :]
+        give_block(k, rows, lhs, 1 - chip)
+        hold[0, rows, :] = product(lhs, 1 - chip, core)
+        if k:
+            reduce_block(k - 1)
+        give_block(k, rows, lhs, chip)
+        if last:
+            reduce_block(k)
+        hold[1, rows, :] = product(lhs, chip, core)
+
     def finish_block(k):
         r0, rn = blocks[k]
         rows = pl.ds(r0, rn)
+        stage1[k][1].wait_recv()
+        partial = hold[1, rows, :] + got1[chip, rows, :]
         stage2[k].wait_recv()
-        total = hold[1, rows, :] + got1[chip, rows, :] + got2[rows, :]
         base = ix * half if k == 0 else (1 - ix) * half + r0
-        nat = pl.ds(pl.multiple_of(base, 32), rn)
-        out_ref[nat, :] = (h_ref[nat, :].astype(F32) + total).astype(BF16)
+        out_ref[pl.ds(pl.multiple_of(base, 16), rn), :] = partial + got2[rows, :]
 
     n_blk = len(blocks)
     for k in range(n_blk):
-        run_block(k)
-        if k:
-            reduce_block(k - 1)
-    reduce_block(n_blk - 1)
+        run_block(k, k == n_blk - 1)
     for k in range(n_blk):
         finish_block(k)
-    for c in sends + stage1 + stage2 + o_copies:
+    for c in sends + [c for g in stage1 for c in g] + stage2 + o_copies:
         c.wait_send()
 
 
-def tail(keeps, recvs, o, hidden, w_down, w_o):
-    rows, width = hidden.shape
+def tail(keeps, recvs, o, rows, width, w_down, w_o):
     n_gu = len(keeps)
     half = keeps[0].shape[1]
     n = w_down.shape[1]
     kdim = w_down.shape[0] + w_o.shape[0]
-    cuts = [(0, 64), (64, 32), (96, 32)]
+    cuts = [(0, 64), (64, 32), (96, 16), (112, 16)]
     n_w, n_cut, n_blk = 8, len(cuts), len(cuts) + 1
     vm = pl.BlockSpec(memory_space=pltpu.VMEM)
-    anywhere = pl.BlockSpec(memory_space=pl.ANY)
+    hbm = pl.BlockSpec(memory_space=pltpu.HBM)
     dma = pltpu.SemaphoreType.DMA
     return pl.pallas_call(
         functools.partial(tail_kernel, n_gu, cuts, n_w),
-        out_shape=jax.ShapeDtypeStruct((rows, width), BF16),
-        in_specs=[anywhere] * (2 * n_gu) + [vm, vm] + [pl.BlockSpec(memory_space=pltpu.HBM)] * 2,
+        out_shape=jax.ShapeDtypeStruct((rows, width), F32),
+        in_specs=[hbm] * (2 * n_gu) + [vm] + [hbm] * 2,
         out_specs=vm,
         scratch_shapes=[
             pltpu.VMEM((kdim, n), BF16),
@@ -620,17 +638,17 @@
             dma((n_cut, n_gu)),
             dma((n_cut,)),
             dma((n_cut,)),
-            dma((n_blk,)),
-            dma((n_blk,)),
+            dma((n_blk, 2)),
+            dma((n_blk, 2)),
             dma((n_blk,)),
             dma((n_blk,)),
             dma((7,)),
             dma((7,)),
         ],
-        compiler_params=pltpu.CompilerParams(collective_id=1, has_side_effects=True, vmem_limit_bytes=56 * 2**20),
+        compiler_params=pltpu.CompilerParams(collective_id=1, has_side_effects=True, vmem_limit_bytes=44 * 2**20),
         cost_estimate=pl.CostEstimate(flops=2 * rows * kdim * n, bytes_accessed=2 * kdim * n, transcendentals=0),
         name="tail",
-    )(*keeps, *recvs, o, hidden, w_down, w_o)
+    )(*keeps, *recvs, o, w_down, w_o)
 
 
 def solution(mesh):
@@ -658,7 +676,8 @@
 
         cos_tab, sin_tab = rope_tables(positions, k_cache.shape[2])
         o, k_all, v_all = attention(q, kv_new, cos_tab, sin_tab, k_cache, v_cache, positions)
-        hidden_out = tail(keep, recv, o, hidden, w_down, w_o)
+        total = tail(keep, recv, o, *hidden.shape, w_down, w_o)
+        hidden_out = (hidden.astype(F32) + total).astype(BF16)
         return hidden_out, k_all, v_all
 
     return jax.shard_map(device_step, mesh=mesh, in_specs=in_specs, out_specs=out_specs, check_vma=False)

time: 164 us -> 161 us (0.982)
  local copies, waits for them, and re-layouts: 2.69 us -> 0.04 us
  Pallas kernels: 139 us -> 137 us
    unnamed x11 -> x20, local copies, waits for them, and re-layouts: 2.69 us -> 0.04 us
where the time goes in v2:
time: 161 us
  Pallas kernels  137 us (85%)
  waiting for transfers between devices  17.9 us (11%)
  starting transfers between devices  4.09 us (3%)
    pallas_call x1, Pallas kernels, attention(): pl.pallas_call(functools.partial(attn_kernel, nb, ahead), out_shape=[jax....  44.7 us
    pallas_call x1, Pallas kernels, tail(): pl.pallas_call(functools.partial(tail_kernel, n_gu, cuts, n_w), out_shape...  41.4 us
    pallas_call x1, Pallas kernels, front(): pl.pallas_call(functools.partial(front_kernel, nx, ny, ge, gc), out_shape...  31.4 us
    pallas_call x3, Pallas kernels, gate_up(): pl.pallas_call(gu_kernel, grid=(cols // blk,), out_shape=[shape, shape],...  19.6 us
    ppermute x4, waiting for transfers between devices, device_step(): recv.append(lax.ppermute(send, 'tpx', swap_x))  17.9 us
    ppermute x4, starting transfers between devices, device_step(): recv.append(lax.ppermute(send, 'tpx', swap_x))  4.09 us
  transfers between devices with their start and end apart: 4, of which 1 were waited for; matrix products, arithmetic and copies ran while one was open for 0% of the time, Pallas kernels for 40%

profile of v2, /device:TPU:0, one launch (start us, length us, event | category | flops | bytes accessed | tf_op | source)
XLA Modules:
  0.0 160.9 jit_solution(3215567219232341833)
XLA Ops:
  0.6 31.4 %front.1 = (f32[4,32,1024]{2,1,0:T(8,128)}, bf16[32,512]{1,0:T(8,128)(2,1)}, f32[2,128,256]{2,1,0:T(8,128)}, f32[2,128,256]{2,1,0:T(8,128)}, bf16[256,2048]{1,0:...) custom-call(bf16[256,512]{1,0:T(8,128)(2,1)} %h_ref.1, f32[1,512]{1,0:T(1,128)} %bitcast.1, ...), custom_call_target="tpu_custom_call" | custom-call | flops 1073741824 | bytes 4194304 | tf_op jit(solution)/shard_map/front/pallas_call | solution.py:250
  32.1 1.1 collective-permute-start
  33.2 6.0 %gate_up.5 = (f32[2,128,768]{2,1,0:T(8,128)}, f32[2,128,768]{2,1,0:T(8,128)}) custom-call(bf16[256,2048]{1,0:T(8,128)(2,1)} %get-tuple-element.21.u_ref, bf16[2048,4096]{1,0:T(8,128)(2,1)} %wg_ref.5, bf16[2048,4096]{1,0:T(8,128)(2,1)} %wu_ref.5), custom_call_target="tpu_custom_call" | custom-call | flops 1610612736 | bytes 6291456 | tf_op jit(solution)/shard_map/gate_up/pallas_call | solution.py:321
  39.2 0.9 collective-permute-start.3
  40.2 6.8 %gate_up.3 = (f32[2,128,1024]{2,1,0:T(8,128)}, f32[2,128,1024]{2,1,0:T(8,128)}) custom-call(bf16[256,2048]{1,0:T(8,128)(2,1)} %get-tuple-element.21.u_ref, bf16[2048,4096]{1,0:T(8,128)(2,1)} %wg_ref.5, bf16[2048,4096]{1,0:T(8,128)(2,1)} %wu_ref.5), custom_call_target="tpu_custom_call" | custom-call | flops 2147483648 | bytes 8388608 | tf_op jit(solution)/shard_map/gate_up/pallas_call | solution.py:321
  47.0 0.0 copy-start.8
  47.0 0.0 copy-start.6
  47.0 0.0 copy-start.7
  47.0 1.1 collective-permute-start.1
  48.1 6.8 %gate_up.4 = (f32[2,128,1024]{2,1,0:T(8,128)}, f32[2,128,1024]{2,1,0:T(8,128)}) custom-call(bf16[256,2048]{1,0:T(8,128)(2,1)} %get-tuple-element.21.u_ref, bf16[2048,4096]{1,0:T(8,128)(2,1)} %wg_ref.5, bf16[2048,4096]{1,0:T(8,128)(2,1)} %wu_ref.5), custom_call_target="tpu_custom_call" | custom-call | flops 2147483648 | bytes 8388608 | tf_op jit(solution)/shard_map/gate_up/pallas_call | solution.py:321
  54.9 0.9 collective-permute-start.2
  55.8 0.0 copy-done.8
  55.8 0.1 multiply_sine_fusion
  56.0 0.0 copy-done.6
  56.0 0.0 copy-done.7
  56.0 0.0 copy-start
  56.0 0.0 copy-start.1
  56.0 0.0 copy-start.2
  56.0 0.0 copy-start.3
  56.0 0.0 copy-start.4
  56.1 0.0 copy-start.5
  56.1 44.7 %attention.1 = (bf16[4,32,1024]{2,1,0:T(8,128)(2,1)S(1)}, bf16[32,2048,256]{2,1,0:T(8,128)(2,1)}, bf16[32,2048,256]{2,1,0:T(8,128)(2,1)}) custom-call(s32[32]{0:T(128)S(1)} %copy-done.8, f32[4,32,1024]{2,1,0:T(8,128)S(1)} %copy-done.6, bf16[32,512]{1,0:T(8,128)(2,1)S(1)} %copy-done.7, f32[32,128]{1,0:T(8,128)S(1)} %get-tuple-element.36.cos_ref, ...), custom_call_target="tpu_custom_call" | custom-call | flops 40000000000 | bytes 134217728 | tf_op jit(solution)/shard_map/attention/pallas_call | solution.py:415
  100.8 0.0 copy-start.9
  100.8 0.0 collective-permute-done.3.refs_9_
  100.8 0.0 collective-permute-done.refs_6_
  100.8 0.0 collective-permute-done.1.refs_7_
  100.8 17.9 %collective-permute-done.2.refs_8_ = f32[2,128,1024]{2,1,0:T(8,128)S(1)} collective-permute-done((f32[2,128,1024]{2,1,0:T(8,128)}, f32[2,128,1024]{2,1,0:T(8,128)S(1)}, u32[]{:S(2)}, u32[]{:S(2)}) %collective-permute-start.2) | collective-permute-done | bytes 1048608 | tf_op jit(solution)/shard_map/ppermute | solution.py:675
  118.7 0.0 copy-done
  118.7 0.0 copy-done.1
  118.7 0.0 copy-done.2
  118.7 0.0 copy-done.3
  118.7 0.0 copy-done.4
  118.7 0.0 copy-done.5
  118.7 41.4 %tail.1 = f32[256,512]{1,0:T(8,128)S(1)} custom-call(f32[2,128,256]{2,1,0:T(8,128)S(1)} %copy-done.4, f32[2,128,1024]{2,1,0:T(8,128)S(1)} %copy-done, f32[2,128,1024]{2,1,0:T(8,128)S(1)} %copy-done.1, f32[2,128,1024]{2,1,0:T(8,128)S(1)} %copy-done.2, f32[2,128,768]{2,1,0:T(8,128)S(1)} %copy-done.3, f32[2,128,256]{2,1,0:T(8,128)S(1)} %copy-done.5, ...), custom_call_target="tpu_custom_call" | custom-call | flops 5368709120 | bytes 20971520 | tf_op jit(solution)/shard_map/tail/pallas_call | solution.py:620
  160.1 0.0 copy-done.9
  160.1 0.8 add_convert_fusion
  (2 shorter events, 0.0 us)
Async XLA Ops:
  32.1 68.7 %collective-permute-start = (f32[2,128,1024]{2,1,0:T(8,128)}, f32[2,128,1024]{2,1,0:T(8,128)S(1)}, u32[]{:S(2)}, u32[]{:S(2)}) collective-permute-start(f32[2,128,1024]{2,1,0:T(8,128)} %get-tuple-element.26), channel_id=1, source_target_pairs={{0,4},{4,0},{1,5},{5,1},{2,6},{6,2},{3,7},{7,3}} | collective-permute-start | bytes 3145736 | tf_op jit(solution)/shard_map/ppermute | solution.py:675
  39.2 61.6 %collective-permute-start.3 = (f32[2,128,768]{2,1,0:T(8,128)}, f32[2,128,768]{2,1,0:T(8,128)S(1)}, u32[]{:S(2)}, u32[]{:S(2)}) collective-permute-start(f32[2,128,768]{2,1,0:T(8,128)} %get-tuple-element.29), channel_id=1, source_target_pairs={{0,4},{4,0},{1,5},{5,1},{2,6},{6,2},{3,7},{7,3}} | collective-permute-start | bytes 2359304 | tf_op jit(solution)/shard_map/ppermute | solution.py:675
  47.0 8.8 %copy-start.8 = (s32[32]{0:T(128)S(1)}, s32[32]{0:T(128)}, u32[]{:S(2)}) copy-start(s32[32]{0:T(128)} %pos_ref.1) | copy-start | bytes 388
  47.0 9.0 %copy-start.6 = (f32[4,32,1024]{2,1,0:T(8,128)S(1)}, f32[4,32,1024]{2,1,0:T(8,128)}, u32[]{:S(2)}) copy-start(f32[4,32,1024]{2,1,0:T(8,128)} %get-tuple-element.30.q_ref) | copy-start | bytes 1572868
  47.0 9.0 %copy-start.7 = (bf16[32,512]{1,0:T(8,128)(2,1)S(1)}, bf16[32,512]{1,0:T(8,128)(2,1)}, u32[]{:S(2)}) copy-start(bf16[32,512]{1,0:T(8,128)(2,1)} %get-tuple-element.31.kv_ref) | copy-start | bytes 98308
  47.0 53.8 %collective-permute-start.1 = (f32[2,128,1024]{2,1,0:T(8,128)}, f32[2,128,1024]{2,1,0:T(8,128)S(1)}, u32[]{:S(2)}, u32[]{:S(2)}) collective-permute-start(f32[2,128,1024]{2,1,0:T(8,128)} %get-tuple-element.27), channel_id=1, source_target_pairs={{0,4},{4,0},{1,5},{5,1},{2,6},{6,2},{3,7},{7,3}} | collective-permute-start | bytes 3145736 | tf_op jit(solution)/shard_map/ppermute | solution.py:675
  54.9 63.8 %collective-permute-start.2 = (f32[2,128,1024]{2,1,0:T(8,128)}, f32[2,128,1024]{2,1,0:T(8,128)S(1)}, u32[]{:S(2)}, u32[]{:S(2)}) collective-permute-start(f32[2,128,1024]{2,1,0:T(8,128)} %get-tuple-element.28), channel_id=1, source_target_pairs={{0,4},{4,0},{1,5},{5,1},{2,6},{6,2},{3,7},{7,3}} | collective-permute-start | bytes 3145736 | tf_op jit(solution)/shard_map/ppermute | solution.py:675
  56.0 62.7 %copy-start = (f32[2,128,1024]{2,1,0:T(8,128)S(1)}, f32[2,128,1024]{2,1,0:T(8,128)}, u32[]{:S(2)}) copy-start(f32[2,128,1024]{2,1,0:T(8,128)} %get-tuple-element.20.refs_1_) | copy-start | bytes 3145732
  56.0 62.7 %copy-start.1 = (f32[2,128,1024]{2,1,0:T(8,128)S(1)}, f32[2,128,1024]{2,1,0:T(8,128)}, u32[]{:S(2)}) copy-start(f32[2,128,1024]{2,1,0:T(8,128)} %get-tuple-element.22.refs_2_) | copy-start | bytes 3145732
  56.0 62.7 %copy-start.2 = (f32[2,128,1024]{2,1,0:T(8,128)S(1)}, f32[2,128,1024]{2,1,0:T(8,128)}, u32[]{:S(2)}) copy-start(f32[2,128,1024]{2,1,0:T(8,128)} %get-tuple-element.23.refs_3_) | copy-start | bytes 3145732
  56.0 62.7 %copy-start.3 = (f32[2,128,768]{2,1,0:T(8,128)S(1)}, f32[2,128,768]{2,1,0:T(8,128)}, u32[]{:S(2)}) copy-start(f32[2,128,768]{2,1,0:T(8,128)} %get-tuple-element.24.refs_4_) | copy-start | bytes 2359300
  56.0 62.7 %copy-start.4 = (f32[2,128,256]{2,1,0:T(8,128)S(1)}, f32[2,128,256]{2,1,0:T(8,128)}, u32[]{:S(2)}) copy-start(f32[2,128,256]{2,1,0:T(8,128)} %get-tuple-element.19.refs_0_) | copy-start | bytes 786436
  56.1 62.7 %copy-start.5 = (f32[2,128,256]{2,1,0:T(8,128)S(1)}, f32[2,128,256]{2,1,0:T(8,128)}, u32[]{:S(2)}) copy-start(f32[2,128,256]{2,1,0:T(8,128)} %get-tuple-element.25.refs_5_) | copy-start | bytes 786436
  100.8 59.3 %copy-start.9 = (bf16[256,512]{1,0:T(8,128)(2,1)S(1)}, bf16[256,512]{1,0:T(8,128)(2,1)}, u32[]{:S(2)}) copy-start(bf16[256,512]{1,0:T(8,128)(2,1)} %h_ref.1) | copy-start | bytes 786436
